TPU v7x, 512 devices: a whole 4x4x16 slice. The times are simulated.
512 devices in a mesh: facet: 64 (over y, z_hi, x), band: 4 (over z_lo), sub: 2 (over core).
Axes of the slice: x: 4, y: 4, z: 16 (z_hi: 4, z_lo: 4; z = z_hi * 4 + z_lo), core: 2. Of those that a mesh axis runs over, the one named last changes fastest.
Arguments:
- facets: bfloat16 [131072, 2048], P(('facet', 'band')), may hold values from -6 to 6
- window: float32 [2048], replicated, may hold values from 0.5 to 1.5
- facet_offsets: int32 [64, 2], replicated, may hold values from 0 to 49151
- row_offsets: int32 [8], replicated, may hold values from 0 to 49151
- column_offset: int32 [1], replicated, may hold values from 0 to 49151
- kernel: bfloat16 [256, 256], replicated, may hold values from -0.375 to 0.375
- tile_counts: int32 [8, 16, 16], replicated, may hold values from 0 to 32
Outputs:
- residual: bfloat16 [131072, 2048], P(('facet', 'band'))
All inputs are finite; a program needn't handle non-finite values.
Results may differ from a plain program's by a relative error of at most 0.013.
Values may be sent and summed in bfloat16 or wider, within the bound.
No kernel may reach another device: no remote copies, remote signals or barrier semaphores. Data moves between devices by JAX's collectives and lax.ppermute only.
A program may use at most 64 MiB of HBM per device.

v0:
```python
import math

import jax
import jax.numpy as jnp
import numpy as np
from jax import lax
from jax.experimental import pallas as pl
from jax.experimental.pallas import tpu as pltpu
from jax.sharding import Mesh
from jax.sharding import PartitionSpec as P

IMAGE = 49152
STEP = 16
PLANE = ("y", "x")
DEPTH = ("zh", "zl")
ROWS = ("y", "zh", "x", "zl")


def wrapped(value):
    return jnp.where(value >= IMAGE, value - IMAGE, value)


def unit_circle(first, second):
    whole = first * second
    upper = lax.shift_right_logical(whole, jnp.int32(14))
    thirds = jnp.floor((upper.astype(jnp.float32) + 0.5) * (1.0 / 3.0)).astype(jnp.int32)
    reduced = (whole & 16383) + ((upper - 3 * thirds) << 14)
    turns = reduced.astype(jnp.float32)
    quarter = jnp.floor(turns * (4.0 / IMAGE) + 0.5)
    angle = (turns - quarter * (IMAGE / 4)) * (2.0 * math.pi / IMAGE)
    q = quarter.astype(jnp.int32)
    z = angle * angle
    sine = angle + angle * z * (
        -1.6666654611e-1 + z * (8.3321608736e-3 + z * -1.9515295891e-4)
    )
    cosine = 1.0 - 0.5 * z + z * z * (
        4.166664568298827e-2 + z * (-1.388731625493765e-3 + z * 2.443315711809948e-5)
    )
    odd = (q & 1) == 1
    c = jnp.where(odd, sine, cosine)
    s = jnp.where(odd, cosine, sine)
    c = jnp.where(((q + 1) & 2) == 2, -c, c)
    s = jnp.where((q & 2) == 2, -s, s)
    return c, s


def iota(shape, dim):
    return lax.broadcasted_iota(jnp.int32, shape, dim)


def nt(a, b):
    return lax.dot_general(a, b, (((1,), (1,)), ((), ())), preferred_element_type=jnp.float32)


def nn(a, b):
    return lax.dot_general(a, b, (((1,), (0,)), ((), ())), preferred_element_type=jnp.float32)


def forward_kernel(
    where_ref, offs_ref, rows_ref, col_ref, window_ref, facet_ref,
    part_ref, a_ref, d_ref, b_scr, t_scr,
    *, bands, subs, per, contrib, a_scale, b_scale, d_scale,
):
    me = where_ref[0]
    facet_at = me // (bands * subs)
    band_at = (me // subs) % bands
    sub_at = me % subs
    ox = offs_ref[facet_at, 0]
    oy = offs_ref[facet_at, 1]
    nx, ny = facet_ref.shape
    blocks = contrib // STEP

    v = wrapped(oy + iota((STEP, ny), 1))
    small_c, small_s = unit_circle(iota((STEP, ny), 0), v)
    big_c, big_s = unit_circle(wrapped(col_ref[0] + STEP * iota((blocks, ny), 0)), v)
    taper = window_ref[...]
    for a in range(blocks):
        gc, gs = big_c[a : a + 1], big_s[a : a + 1]
        c = gc * small_c - gs * small_s
        s = gc * small_s + gs * small_c
        lo = a * STEP
        b_scr[lo : lo + STEP, :] = (c * taper * b_scale).astype(jnp.bfloat16)
        b_scr[contrib + lo : contrib + lo + STEP, :] = (-s * taper * b_scale).astype(jnp.bfloat16)
        d_ref[lo : lo + STEP, :] = (c * d_scale).astype(jnp.bfloat16)
        d_ref[contrib + lo : contrib + lo + STEP, :] = (-s * d_scale).astype(jnp.bfloat16)
    t = nt(b_scr[...], facet_ref[...])
    tr = t[:contrib].astype(jnp.bfloat16)
    ti = t[contrib:].astype(jnp.bfloat16)
    t_scr[0, :contrib, :] = tr
    t_scr[0, contrib:, :] = ti
    t_scr[1, :contrib, :] = -ti
    t_scr[1, contrib:, :] = tr

    v = wrapped(ox + band_at * nx + iota((STEP, nx), 1))
    small_c, small_s = unit_circle(iota((STEP, nx), 0), v)
    small_c = small_c * a_scale
    small_s = small_s * a_scale
    for s_at in range(per):
        start = rows_ref[sub_at * per + s_at]
        big_c, big_s = unit_circle(wrapped(start + STEP * iota((blocks, nx), 0)), v)
        for a in range(blocks):
            gc, gs = big_c[a : a + 1], big_s[a : a + 1]
            c = gc * small_c - gs * small_s
            s = gc * small_s + gs * small_c
            a_ref[s_at, 0, a * STEP : (a + 1) * STEP, :] = c.astype(jnp.bfloat16)
            a_ref[s_at, 1, a * STEP : (a + 1) * STEP, :] = (-s).astype(jnp.bfloat16)
        part = nt(t_scr[0], a_ref[s_at, 0]) + nt(t_scr[1], a_ref[s_at, 1])
        part_ref[0, s_at] = part[:contrib].astype(jnp.bfloat16)
        part_ref[1, s_at] = part[contrib:].astype(jnp.bfloat16)


def middle_kernel(
    where_ref, grid_ref, a_ref, kern_ref, kern_t_ref, counts_ref, e_ref,
    y_scr, w_scr, r_scr, *, subs, per, contrib, tile,
):
    sub_at = where_ref[0] % subs
    tiles = contrib // tile
    k = kern_ref[...]
    kt = kern_t_ref[...]
    spread = (iota((tiles, contrib), 1) // tile == iota((tiles, contrib), 0)).astype(jnp.bfloat16)
    for c in range(2):
        for s in range(per):
            y_scr[c, s] = nn(k, grid_ref[c, s]).astype(jnp.bfloat16)
    for s in range(per):
        count = nn(counts_ref[sub_at * per + s], spread)
        weight = (count / (count + 4.0))[:, None, :]
        for c in range(2):
            z = nt(y_scr[c, s], k).reshape(tiles, tile, contrib)
            w_scr[c, s] = (weight * z).reshape(contrib, contrib).astype(jnp.bfloat16)
    for s in range(per):
        for c in range(2):
            u = nn(w_scr[c, s], k).astype(jnp.bfloat16)
            r_scr[s, c] = nn(kt, u).astype(jnp.bfloat16)
    total = None
    for s in range(per):
        rr = r_scr[s, 0]
        ri = r_scr[s, 1]
        here = nn(jnp.concatenate([rr, ri], 0), a_ref[s, 0])
        here = here + nn(jnp.concatenate([ri, -rr], 0), a_ref[s, 1])
        total = here if total is None else total + here
    e_ref[...] = total.T.astype(jnp.bfloat16)


def backward_kernel(mine_ref, other_ref, d_ref, window_ref, out_ref):
    e = (mine_ref[...].astype(jnp.float32) + other_ref[...].astype(jnp.float32)).astype(jnp.bfloat16)
    image = nn(e, d_ref[...])
    out_ref[...] = (window_ref[...] * image).astype(jnp.bfloat16)


def exchanged(x, axes):
    return lax.all_to_all(x, axes, 0, 0, tiled=True)


def summed(x):
    return jnp.sum(x.astype(jnp.float32), axis=0).astype(jnp.bfloat16)


def body(facets, window, facet_offsets, row_offsets, column_offset, kernel, tile_counts):
    bands, subs = lax.axis_size("zl"), lax.axis_size("core")
    plane, depth = lax.axis_size(PLANE), lax.axis_size(DEPTH)
    facet_count = plane * depth // bands
    nx, ny = facets.shape
    contrib = kernel.shape[0]
    per = row_offsets.shape[0] // subs
    tile = contrib // tile_counts.shape[1]
    a_scale = 1.0 / math.sqrt(ny * facet_count)
    b_scale = 1.0 / math.sqrt(ny)
    back_scale = 1.0 / math.sqrt(row_offsets.shape[0] * contrib)
    d_scale = back_scale / a_scale / math.sqrt(contrib)
    here = lax.axis_index(ROWS + ("core",)).astype(jnp.int32).reshape(1)
    taper = window.reshape(1, ny)
    smem = pl.BlockSpec(memory_space=pltpu.SMEM)
    vmem = pl.BlockSpec(memory_space=pltpu.VMEM)

    part, a_table, d_table = pl.pallas_call(
        lambda *refs: forward_kernel(
            *refs, bands=bands, subs=subs, per=per, contrib=contrib,
            a_scale=a_scale, b_scale=b_scale, d_scale=d_scale,
        ),
        out_shape=(
            jax.ShapeDtypeStruct((2, per, contrib, contrib), jnp.bfloat16),
            jax.ShapeDtypeStruct((per, 2, contrib, nx), jnp.bfloat16),
            jax.ShapeDtypeStruct((2 * contrib, ny), jnp.bfloat16),
        ),
        in_specs=[smem, smem, smem, smem, vmem, vmem],
        out_specs=(vmem, vmem, vmem),
        scratch_shapes=[
            pltpu.VMEM((2 * contrib, ny), jnp.bfloat16),
            pltpu.VMEM((2, 2 * contrib, nx), jnp.bfloat16),
        ],
        name="forward",
    )(here, facet_offsets, row_offsets, column_offset, taper, facets)

    lines = 2 * per * contrib
    mine = summed(exchanged(part.reshape(plane, lines // plane, contrib), PLANE))
    mine = summed(exchanged(mine.reshape(depth, lines // plane // depth, contrib), DEPTH))
    mine = exchanged(jnp.broadcast_to(mine, (depth, *mine.shape)), DEPTH)
    mine = mine.reshape(lines // plane, contrib)
    grid = exchanged(jnp.broadcast_to(mine, (plane, *mine.shape)), PLANE)
    grid = grid.reshape(2, per, contrib, contrib)

    counts = jnp.swapaxes(tile_counts, 1, 2).astype(jnp.bfloat16)
    e_part = pl.pallas_call(
        lambda *refs: middle_kernel(*refs, subs=subs, per=per, contrib=contrib, tile=tile),
        out_shape=jax.ShapeDtypeStruct((nx, 2 * contrib), jnp.bfloat16),
        in_specs=[smem, vmem, vmem, vmem, vmem, vmem],
        out_specs=vmem,
        scratch_shapes=[
            pltpu.VMEM((2, per, contrib, contrib), jnp.bfloat16),
            pltpu.VMEM((2, per, contrib, contrib), jnp.bfloat16),
            pltpu.VMEM((per, 2, contrib, contrib), jnp.bfloat16),
        ],
        name="middle",
    )(here, grid, a_table, kernel, kernel.T, counts)

    other = lax.ppermute(e_part, "core", [(i, (i + 1) % subs) for i in range(subs)])
    step = nx // 4
    return pl.pallas_call(
        backward_kernel,
        out_shape=jax.ShapeDtypeStruct((nx, ny), jnp.bfloat16),
        grid=(nx // step,),
        in_specs=[
            pl.BlockSpec((step, 2 * contrib), lambda i: (i, 0)),
            pl.BlockSpec((step, 2 * contrib), lambda i: (i, 0)),
            pl.BlockSpec((2 * contrib, ny), lambda i: (0, 0)),
            pl.BlockSpec((1, ny), lambda i: (0, 0)),
        ],
        out_specs=pl.BlockSpec((step, ny), lambda i: (i, 0)),
        name="backward",
    )(e_part, other, d_table, taper)


def solution(mesh):
    fine = Mesh(np.asarray(mesh.devices).reshape(4, 4, 4, 4, 2), ROWS + ("core",))
    rows = P(ROWS, None)
    return jax.shard_map(
        body,
        mesh=fine,
        in_specs=(rows, P(), P(), P(), P(), P(), P()),
        out_specs=rows,
        check_vma=False,
    )
```

profile of v0, /device:TPU:1, one launch (start us, length us, event | category | flops | bytes accessed | tf_op | source)
XLA Modules:
  0.0 113.9 jit_solution(17620422174989965840)
XLA Ops:
  0.0 1.4 %copy.11.refs_1_ = s32[64,2]{1,0:T(8,128)} copy(s32[64,2]{0,1:T(2,128)} %param.9) | data formatting | bytes 1024 | tf_op args[2]
  2.1 7.5 %forward.1 = (bf16[2,4,256,256]{3,2,1,0:T(8,128)(2,1)}, bf16[4,2,256,512]{3,2,1,0:T(8,128)(2,1)}, bf16[512,2048]{1,0:T(8,128)(2,1)}) custom-call(s32[1]{0:T(128)} %bitcast.refs_0_, s32[64,2]{1,0:T(8,128)} %copy.11.refs_1_, s32[8]{0:T(128)} %refs_2_.1, s32[1]{0:T(128)S(6)} %copy.14.refs_3_, f32[1,2048]{1,0:T(1,128)} %bitcast.14, bf16[512,2048]{1,0:T(8,128)(2,1)} %refs_5_.1), custom_call_target="tpu_custom_call" | custom-call | tf_op jit(solution)/shard_map/forward/pallas_call | solution.py:175
  9.6 21.7 %all_to_all.20 = bf16[16,128,256]{2,1,0:T(8,128)(2,1)S(1)} all-to-all(bf16[16,128,256]{2,1,0:T(8,128)(2,1)} %bitcast.10), channel_id=1, replica_groups=mesh['y'=4,'zh'=4,'x'=4,'zl'=4,'core'=2] {'y','x'}, dimensions={0} | all-to-all | bytes 2097152 | tf_op jit(solution)/shard_map/all_to_all | solution.py:151
  31.3 0.0 copy-start.2
  31.3 0.1 reduce_sum.24
  31.5 0.0 copy-start.3
  31.5 28.3 %all_to_all.21 = bf16[16,8,256]{2,1,0:T(8,128)(2,1)S(1)} all-to-all(bf16[16,8,256]{2,1,0:T(8,128)(2,1)S(1)} %bitcast.12), channel_id=1, replica_groups=mesh['y'=4,'zh'=4,'x'=4,'zl'=4,'core'=2] {'zh','zl'}, dimensions={0} | all-to-all | bytes 131072 | tf_op jit(solution)/shard_map/all_to_all | solution.py:151
  59.8 14.4 %all_to_all.22 = bf16[16,8,256]{2,1,0:T(8,128)(2,1)S(1)} all-to-all(bf16[16,8,256]{2,1,0:T(8,128)(2,1)S(1)} %broadcast_in_dim.6), channel_id=1, replica_groups=mesh['y'=4,'zh'=4,'x'=4,'zl'=4,'core'=2] {'zh','zl'}, dimensions={0} | all-to-all | bytes 131072 | tf_op jit(solution)/shard_map/all_to_all | solution.py:151
  74.2 1.1 broadcast_in_dim.7
  75.3 3.7 %all-to-all-start.3 = ((bf16[16,128,256]{2,1,0:T(8,128)(2,1)}), bf16[16,128,256]{2,1,0:T(8,128)(2,1)S(1)}, u32[]{:S(2)}, u32[]{:S(2)}) async-start(bf16[16,128,256]{2,1,0:T(8,128)(2,1)} %broadcast_in_dim.7), calls=%async_computation.3 | async-start | bytes 2097152 | tf_op jit(solution)/shard_map/all_to_all | solution.py:151
  79.0 0.0 copy-done.2
  79.0 0.8 copy.12
  79.8 0.0 copy-done.3
  79.8 0.1 copy.13
  79.8 0.6 convert_bitcast_fusion.refs_5_
  80.5 11.9 %all-to-all-done.3 = bf16[16,128,256]{2,1,0:T(8,128)(2,1)S(1)} async-done(((bf16[16,128,256]{2,1,0:T(8,128)(2,1)}), bf16[16,128,256]{2,1,0:T(8,128)(2,1)S(1)}, u32[]{:S(2)}, u32[]{:S(2)}) %all-to-all-start.3) | async-done | bytes 1048608 | tf_op jit(solution)/shard_map/all_to_all | solution.py:151
  92.3 0.0 copy-start
  92.3 1.0 copy-done
  93.3 5.5 %middle.1.mine_ref = bf16[512,512]{1,0:T(8,128)(2,1)} custom-call(s32[1]{0:T(128)} %bitcast.refs_0_, bf16[2,4,256,256]{3,2,1,0:T(8,128)(2,1)} %bitcast.9, bf16[4,2,256,512]{3,2,1,0:T(8,128)(2,1)} %get-tuple-element.9.refs_2_, bf16[256,256]{1,0:T(8,128)(2,1)} %refs_3_.2, bf16[256,256]{1,0:T(8,128)(2,1)} %bitcast.11, ...), custom_call_target="tpu_custom_call" | custom-call | tf_op jit(solution)/shard_map/middle/pallas_call | solution.py:203
  98.8 7.4 %collective-permute-start = (bf16[512,512]{1,0:T(8,128)(2,1)}, bf16[512,512]{1,0:T(8,128)(2,1)S(1)}, u32[]{:S(2)}, u32[]{:S(2)}) collective-permute-start(bf16[512,512]{1,0:T(8,128)(2,1)} %middle.1.mine_ref), channel_id=1, source_target_pairs={{0,1},{1,0},{2,3},{3,2},{4,5},{5,4},{6,7},{7,6},{8,9},{9,8},{10,11... | collective-permute-start | bytes 1572872 | tf_op jit(solution)/shard_map/ppermute | solution.py:216
  106.2 1.7 %collective-permute-done.other_ref = bf16[512,512]{1,0:T(8,128)(2,1)S(1)} collective-permute-done((bf16[512,512]{1,0:T(8,128)(2,1)}, bf16[512,512]{1,0:T(8,128)(2,1)S(1)}, u32[]{:S(2)}, u32[]{:S(2)}) %collective-permute-start) | collective-permute-done | bytes 524320 | tf_op jit(solution)/shard_map/ppermute | solution.py:216
  107.9 0.0 copy-start.1
  107.9 0.8 copy-done.1
  108.7 5.2 %backward.1 = bf16[512,2048]{1,0:T(8,128)(2,1)} custom-call(bf16[512,512]{1,0:T(8,128)(2,1)} %middle.1.mine_ref, bf16[512,512]{1,0:T(8,128)(2,1)} %copy-done.1, bf16[512,2048]{1,0:T(8,128)(2,1)} %get-tuple-element.10.d_ref, f32[1,2048]{1,0:T(1,128)} %bitcast.15), custom_call_target="tpu_custom_call" | custom-call | tf_op jit(solution)/shard_map/backward/pallas_call | solution.py:218
  (2 shorter events, 0.0 us)
Async XLA Ops:
  31.3 47.7 %copy-start.2 = (bf16[256,256]{1,0:T(8,128)(2,1)S(1)}, bf16[256,256]{1,0:T(8,128)(2,1)}, u32[]{:S(2)}) copy-start(bf16[256,256]{1,0:T(8,128)(2,1)} %refs_3_.2) | copy-start | bytes 393220
  31.5 48.3 %copy-start.3 = (s32[8,16,16]{2,1,0:T(8,128)S(1)}, s32[8,16,16]{2,1,0:T(8,128)}, u32[]{:S(2)}) copy-start(s32[8,16,16]{2,1,0:T(8,128)} %param.13) | copy-start | bytes 24580
  75.3 17.0 %all-to-all-start.3 = ((bf16[16,128,256]{2,1,0:T(8,128)(2,1)}), bf16[16,128,256]{2,1,0:T(8,128)(2,1)S(1)}, u32[]{:S(2)}, u32[]{:S(2)}) async-start(bf16[16,128,256]{2,1,0:T(8,128)(2,1)} %broadcast_in_dim.7), calls=%async_computation.3 | async-start | bytes 2097152 | tf_op jit(solution)/shard_map/all_to_all | solution.py:151
  92.3 1.0 copy-start
  98.8 9.1 %collective-permute-start = (bf16[512,512]{1,0:T(8,128)(2,1)}, bf16[512,512]{1,0:T(8,128)(2,1)S(1)}, u32[]{:S(2)}, u32[]{:S(2)}) collective-permute-start(bf16[512,512]{1,0:T(8,128)(2,1)} %middle.1.mine_ref), channel_id=1, source_target_pairs={{0,1},{1,0},{2,3},{3,2},{4,5},{5,4},{6,7},{7,6},{8,9},{9,8},{10,11... | collective-permute-start | bytes 1572872 | tf_op jit(solution)/shard_map/ppermute | solution.py:216
  107.9 0.8 copy-start.1
where the time goes:
time: 114 us
  blocking collectives  64.4 us (56%)
  Pallas kernels  18.2 us (16%)
  waiting for transfers between devices  13.6 us (12%)
  starting transfers between devices  11 us (10%)
  local copies, waits for them, and re-layouts  5.12 us (4%)
    all_to_all x3, blocking collectives, exchanged(): return lax.all_to_all(x, axes, 0, 0, tiled=True)  64.4 us
    all_to_all x1, waiting for transfers between devices, exchanged(): return lax.all_to_all(x, axes, 0, 0, tiled=True)  11.9 us
    pallas_call x1, Pallas kernels, body(): pl.pallas_call(lambda *refs: forward_kernel(*refs, bands=bands, subs=subs...  7.54 us
    ppermute x1, starting transfers between devices, body(): lax.ppermute(e_part, 'core', [(i, (i + 1) % subs) for i in range(subs)])  7.39 us
    pallas_call x1, Pallas kernels, body(): pl.pallas_call(lambda *refs: middle_kernel(*refs, subs=subs, per=per, con...  5.45 us
    pallas_call x1, Pallas kernels, body(): pl.pallas_call(backward_kernel, out_shape=jax.ShapeDtypeStruct((nx, ny),...  5.24 us
    unnamed x11, local copies, waits for them, and re-layouts  4.01 us
    all_to_all x1, starting transfers between devices, exchanged(): return lax.all_to_all(x, axes, 0, 0, tiled=True)  3.65 us
  transfers between devices with their start and end apart: 2, of which 2 were waited for; matrix products, arithmetic and copies ran while one was open for 1% of the time, Pallas kernels for 0%

commit v1 on v0

v1 whole, which is shorter than its diff:
```python
import math

import jax
import jax.numpy as jnp
import numpy as np
from jax import lax
from jax.experimental import pallas as pl
from jax.experimental.pallas import tpu as pltpu
from jax.sharding import Mesh
from jax.sharding import PartitionSpec as P

IMAGE = 49152
STEP = 16
PLANE = ("y", "x")
DEPTH = ("zh", "zl")
ROWS = ("y", "zh", "x", "zl")


def wrapped(value):
    return jnp.where(value >= IMAGE, value - IMAGE, value)


def unit_circle(first, second):
    whole = first * second
    upper = lax.shift_right_logical(whole, jnp.int32(14))
    thirds = jnp.floor((upper.astype(jnp.float32) + 0.5) * (1.0 / 3.0)).astype(jnp.int32)
    reduced = (whole & 16383) + ((upper - 3 * thirds) << 14)
    turns = reduced.astype(jnp.float32)
    quarter = jnp.floor(turns * (4.0 / IMAGE) + 0.5)
    angle = (turns - quarter * (IMAGE / 4)) * (2.0 * math.pi / IMAGE)
    q = quarter.astype(jnp.int32)
    z = angle * angle
    sine = angle + angle * z * (
        -1.6666654611e-1 + z * (8.3321608736e-3 + z * -1.9515295891e-4)
    )
    cosine = 1.0 - 0.5 * z + z * z * (
        4.166664568298827e-2 + z * (-1.388731625493765e-3 + z * 2.443315711809948e-5)
    )
    odd = (q & 1) == 1
    c = jnp.where(odd, sine, cosine)
    s = jnp.where(odd, cosine, sine)
    c = jnp.where(((q + 1) & 2) == 2, -c, c)
    s = jnp.where((q & 2) == 2, -s, s)
    return c, s


def iota(shape, dim):
    return lax.broadcasted_iota(jnp.int32, shape, dim)


def nt(a, b):
    return lax.dot_general(a, b, (((1,), (1,)), ((), ())), preferred_element_type=jnp.float32)


def nn(a, b):
    return lax.dot_general(a, b, (((1,), (0,)), ((), ())), preferred_element_type=jnp.float32)


def turned(big_c, big_s, a, small_c, small_s):
    gc, gs = big_c[a : a + 1], big_s[a : a + 1]
    return gc * small_c - gs * small_s, gc * small_s + gs * small_c


def place(where_ref, bands, subs):
    me = where_ref[0]
    return me // (bands * subs), (me // subs) % bands, me % subs


def column_factors(oy, start, blocks, ny):
    v = wrapped(oy + iota((STEP, ny), 1))
    return unit_circle(iota((STEP, ny), 0), v), unit_circle(
        wrapped(start + STEP * iota((blocks, ny), 0)), v
    )


def row_table(start, v, small, blocks, store):
    big_c, big_s = unit_circle(wrapped(start + STEP * iota((blocks, v.shape[1]), 0)), v)
    for a in range(blocks):
        c, s = turned(big_c, big_s, a, *small)
        store(a * STEP, c.astype(jnp.bfloat16), (-s).astype(jnp.bfloat16))


def forward_kernel(
    where_ref, offs_ref, rows_ref, col_ref, window_ref, facet_hbm,
    part_ref, facet_scr, b_scr, t_scr, a_scr, sem,
    *, bands, subs, per, contrib, a_scale, b_scale,
):
    load = pltpu.make_async_copy(facet_hbm, facet_scr, sem)
    load.start()
    facet_at, band_at, sub_at = place(where_ref, bands, subs)
    ox = offs_ref[0, facet_at]
    oy = offs_ref[1, facet_at]
    nx, ny = facet_scr.shape
    blocks = contrib // STEP

    small, (big_c, big_s) = column_factors(oy, col_ref[0], blocks, ny)
    taper = window_ref[...] * b_scale
    small = (small[0] * taper, small[1] * taper)
    for a in range(blocks):
        c, s = turned(big_c, big_s, a, *small)
        lo = a * STEP
        b_scr[lo : lo + STEP, :] = c.astype(jnp.bfloat16)
        b_scr[contrib + lo : contrib + lo + STEP, :] = (-s).astype(jnp.bfloat16)
    load.wait()
    t = nt(b_scr[...], facet_scr[...])
    tr = t[:contrib].astype(jnp.bfloat16)
    ti = t[contrib:].astype(jnp.bfloat16)
    t_scr[0, :contrib, :] = tr
    t_scr[0, contrib:, :] = ti
    t_scr[1, :contrib, :] = -ti
    t_scr[1, contrib:, :] = tr

    v = wrapped(ox + band_at * nx + iota((STEP, nx), 1))
    small_c, small_s = unit_circle(iota((STEP, nx), 0), v)
    small = (small_c * a_scale, small_s * a_scale)
    for s_at in range(per):

        def store(lo, c, s):
            a_scr[s_at, 0, lo : lo + STEP, :] = c
            a_scr[s_at, 1, lo : lo + STEP, :] = s

        row_table(rows_ref[sub_at * per + s_at], v, small, blocks, store)
    for s_at in range(per):
        part = nt(t_scr[0], a_scr[s_at, 0]) + nt(t_scr[1], a_scr[s_at, 1])
        part_ref[0, s_at] = part[:contrib].astype(jnp.bfloat16)
        part_ref[1, s_at] = part[contrib:].astype(jnp.bfloat16)


def tables_kernel(
    where_ref, offs_ref, rows_ref, col_ref, kern_ref, after_ref, a_ref, d_ref, kern_t_ref,
    *, bands, subs, per, contrib, a_scale, d_scale,
):
    del after_ref
    facet_at, band_at, sub_at = place(where_ref, bands, subs)
    ox = offs_ref[0, facet_at]
    oy = offs_ref[1, facet_at]
    nx, ny = a_ref.shape[3], d_ref.shape[1]
    blocks = contrib // STEP
    kern_t_ref[...] = kern_ref[...].astype(jnp.float32).T.astype(jnp.bfloat16)
    small, (big_c, big_s) = column_factors(oy, col_ref[0], blocks, ny)
    small = (small[0] * d_scale, small[1] * d_scale)
    for a in range(blocks):
        c, s = turned(big_c, big_s, a, *small)
        lo = a * STEP
        d_ref[lo : lo + STEP, :] = c.astype(jnp.bfloat16)
        d_ref[contrib + lo : contrib + lo + STEP, :] = (-s).astype(jnp.bfloat16)
    v = wrapped(ox + band_at * nx + iota((STEP, nx), 1))
    small_c, small_s = unit_circle(iota((STEP, nx), 0), v)
    small = (small_c * a_scale, small_s * a_scale)
    for s_at in range(per):

        def store(lo, c, s):
            a_ref[s_at, 0, lo : lo + STEP, :] = c
            a_ref[s_at, 1, lo : lo + STEP, :] = s

        row_table(rows_ref[sub_at * per + s_at], v, small, blocks, store)


def middle_kernel(
    where_ref, grid_ref, a_hbm, kern_ref, kern_t_ref, counts_ref, e_ref,
    a_ref, y_scr, w_scr, r_scr, sem, *, subs, per, contrib, tile,
):
    load = pltpu.make_async_copy(a_hbm, a_ref, sem)
    load.start()
    sub_at = where_ref[0] % subs
    tiles = contrib // tile
    k = kern_ref[...]
    kt = kern_t_ref[...]
    spread = (iota((tiles, contrib), 1) // tile == iota((tiles, contrib), 0)).astype(jnp.bfloat16)
    for c in range(2):
        for s in range(per):
            y_scr[c, s] = nn(k, grid_ref[c, s]).astype(jnp.bfloat16)
    for s in range(per):
        count = nn(counts_ref[sub_at * per + s], spread)
        weight = (count / (count + 4.0))[:, None, :]
        for c in range(2):
            z = nt(y_scr[c, s], k).reshape(tiles, tile, contrib)
            w_scr[c, s] = (weight * z).reshape(contrib, contrib).astype(jnp.bfloat16)
    for s in range(per):
        for c in range(2):
            u = nn(w_scr[c, s], k).astype(jnp.bfloat16)
            r_scr[s, c] = nn(kt, u).astype(jnp.bfloat16)
    load.wait()
    total = None
    for s in range(per):
        rr = r_scr[s, 0]
        ri = r_scr[s, 1]
        here = nn(jnp.concatenate([rr, ri], 0), a_ref[s, 0])
        here = here + nn(jnp.concatenate([ri, -rr], 0), a_ref[s, 1])
        total = here if total is None else total + here
    e_ref[...] = total.T.astype(jnp.bfloat16)


def backward_kernel(mine_ref, other_ref, d_ref, window_ref, out_ref, e_scr, *, cols):
    at = pl.program_id(0)

    @pl.when(at == 0)
    def _():
        e_scr[...] = (
            mine_ref[...].astype(jnp.float32) + other_ref[...].astype(jnp.float32)
        ).astype(jnp.bfloat16)

    here = pl.ds(pl.multiple_of(at * cols, cols), cols)
    image = nn(e_scr[...], d_ref[:, here])
    out_ref[...] = (window_ref[:, here] * image).astype(jnp.bfloat16)


def exchanged(x, axes):
    return lax.all_to_all(x, axes, 0, 0, tiled=True)


def summed(x):
    return jnp.sum(x.astype(jnp.float32), axis=0).astype(jnp.bfloat16)


def near(x):
    return pltpu.with_memory_space_constraint(x, pltpu.VMEM)


def body(facets, window, facet_offsets, row_offsets, column_offset, kernel, tile_counts):
    bands, subs = lax.axis_size("zl"), lax.axis_size("core")
    plane, depth = lax.axis_size(PLANE), lax.axis_size(DEPTH)
    facet_count = plane * depth // bands
    nx, ny = facets.shape
    contrib = kernel.shape[0]
    per = row_offsets.shape[0] // subs
    tile = contrib // tile_counts.shape[1]
    a_scale = 1.0 / math.sqrt(ny * facet_count)
    b_scale = 1.0 / math.sqrt(ny)
    back_scale = 1.0 / math.sqrt(row_offsets.shape[0] * contrib)
    d_scale = back_scale / a_scale / math.sqrt(contrib)
    here = lax.axis_index(ROWS + ("core",)).astype(jnp.int32).reshape(1)
    taper = window.reshape(1, ny)
    offsets = facet_offsets.T
    smem = pl.BlockSpec(memory_space=pltpu.SMEM)
    vmem = pl.BlockSpec(memory_space=pltpu.VMEM)
    anywhere = pl.BlockSpec(memory_space=pl.ANY)
    far = pl.BlockSpec(memory_space=pltpu.HBM)

    part = pl.pallas_call(
        lambda *refs: forward_kernel(
            *refs, bands=bands, subs=subs, per=per, contrib=contrib, a_scale=a_scale, b_scale=b_scale,
        ),
        out_shape=pltpu.VMEM((2, per, contrib, contrib), jnp.bfloat16),
        in_specs=[smem, smem, smem, smem, vmem, far],
        out_specs=vmem,
        scratch_shapes=[
            pltpu.VMEM((nx, ny), jnp.bfloat16),
            pltpu.VMEM((2 * contrib, ny), jnp.bfloat16),
            pltpu.VMEM((2, 2 * contrib, nx), jnp.bfloat16),
            pltpu.VMEM((per, 2, contrib, nx), jnp.bfloat16),
            pltpu.SemaphoreType.DMA(()),
        ],
        compiler_params=pltpu.CompilerParams(vmem_limit_bytes=28 * 2**20),
        name="forward",
    )(here, offsets, row_offsets, column_offset, taper, pltpu.with_memory_space_constraint(facets, pltpu.HBM))

    lines = 2 * per * contrib
    mine = summed(exchanged(part.reshape(plane, lines // plane, contrib), PLANE))
    a_table, d_table, kernel_t = pl.pallas_call(
        lambda *refs: tables_kernel(
            *refs, bands=bands, subs=subs, per=per, contrib=contrib, a_scale=a_scale, d_scale=d_scale,
        ),
        out_shape=(
            pltpu.HBM((per, 2, contrib, nx), jnp.bfloat16),
            pltpu.VMEM((2 * contrib, ny), jnp.bfloat16),
            pltpu.VMEM((contrib, contrib), jnp.bfloat16),
        ),
        in_specs=[smem, smem, smem, smem, vmem, anywhere],
        out_specs=(vmem, vmem, vmem),
        cost_estimate=pl.CostEstimate(flops=6_000_000_000, transcendentals=0, bytes_accessed=4_000_000),
        compiler_params=pltpu.CompilerParams(vmem_limit_bytes=20 * 2**20),
        name="tables",
    )(here, offsets, row_offsets, column_offset, kernel, mine)
    mine = summed(exchanged(mine.reshape(depth, lines // plane // depth, contrib), DEPTH))
    mine = exchanged(jnp.broadcast_to(mine, (depth, *mine.shape)), DEPTH)
    mine = mine.reshape(lines // plane, contrib)
    grid = exchanged(jnp.broadcast_to(mine, (plane, *mine.shape)), PLANE)
    grid = grid.reshape(2, per, contrib, contrib)

    counts = jnp.swapaxes(tile_counts, 1, 2).astype(jnp.bfloat16)
    e_part = pl.pallas_call(
        lambda *refs: middle_kernel(*refs, subs=subs, per=per, contrib=contrib, tile=tile),
        out_shape=pltpu.VMEM((nx, 2 * contrib), jnp.bfloat16),
        in_specs=[smem, vmem, far, vmem, vmem, vmem],
        out_specs=vmem,
        scratch_shapes=[
            pltpu.VMEM((per, 2, contrib, nx), jnp.bfloat16),
            pltpu.VMEM((2, per, contrib, contrib), jnp.bfloat16),
            pltpu.VMEM((2, per, contrib, contrib), jnp.bfloat16),
            pltpu.VMEM((per, 2, contrib, contrib), jnp.bfloat16),
            pltpu.SemaphoreType.DMA(()),
        ],
        compiler_params=pltpu.CompilerParams(vmem_limit_bytes=28 * 2**20),
        name="middle",
    )(here, near(grid), pltpu.with_memory_space_constraint(a_table, pltpu.HBM), kernel, near(kernel_t), counts)

    other = lax.ppermute(e_part, "core", [(i, (i + 1) % subs) for i in range(subs)])
    cols = ny // 4
    return pl.pallas_call(
        lambda *refs: backward_kernel(*refs, cols=cols),
        out_shape=jax.ShapeDtypeStruct((nx, ny), jnp.bfloat16),
        grid=(ny // cols,),
        in_specs=[vmem, vmem, vmem, vmem],
        out_specs=pl.BlockSpec((nx, cols), lambda i: (0, i)),
        scratch_shapes=[pltpu.VMEM((nx, 2 * contrib), jnp.bfloat16)],
        compiler_params=pltpu.CompilerParams(vmem_limit_bytes=28 * 2**20),
        name="backward",
    )(near(e_part), near(other), near(d_table), taper)


def solution(mesh):
    fine = Mesh(np.asarray(mesh.devices).reshape(4, 4, 4, 4, 2), ROWS + ("core",))
    rows = P(ROWS, None)
    return jax.shard_map(
        body,
        mesh=fine,
        in_specs=(rows, P(), P(), P(), P(), P(), P()),
        out_specs=rows,
        check_vma=False,
    )
```

time: 114 us -> 107 us (0.939)
  waiting for transfers between devices: 13.6 us -> 9.97 us
  local copies, waits for them, and re-layouts: 5.12 us -> 3.21 us
    all_to_all x1, waiting for transfers between devices: 11.9 us -> 8.45 us  [exchanged(): return lax.all_to_all(x, axes, 0, 0, tiled=True)]
    pallas_call x1 -> x2, Pallas kernels: 5.24 us -> 7.81 us  [the longest x1 4.76 us: body(): pl.pallas_call(lambda *refs: tables_kernel(*refs, bands=bands, subs=subs,...]
    pallas_call x1, Pallas kernels: 7.54 us -> 5.01 us  [body(): pl.pallas_call(lambda *refs: forward_kernel(*refs, bands=bands, subs=subs...]
    unnamed x11 -> x17, local copies, waits for them, and re-layouts: 4.01 us -> 2.13 us
  transfers between devices with their start and end apart: 2 -> 2, of which waited for: 2 -> 2; matrix products, arithmetic and copies ran while one was open for 1% -> 0% of each run, Pallas kernels for 0% -> 4%
where the time goes in v1:
time: 107 us
  blocking collectives  64.2 us (60%)
  Pallas kernels  17.2 us (16%)
  starting transfers between devices  11.1 us (10%)
  waiting for transfers between devices  9.97 us (9%)
  local copies, waits for them, and re-layouts  3.21 us (3%)
    all_to_all x3, blocking collectives, exchanged(): return lax.all_to_all(x, axes, 0, 0, tiled=True)  64.2 us
    all_to_all x1, waiting for transfers between devices, exchanged(): return lax.all_to_all(x, axes, 0, 0, tiled=True)  8.45 us
    ppermute x1, starting transfers between devices, body(): lax.ppermute(e_part, 'core', [(i, (i + 1) % subs) for i in range(subs)])  7.41 us
    pallas_call x1, Pallas kernels, body(): pl.pallas_call(lambda *refs: forward_kernel(*refs, bands=bands, subs=subs...  5.01 us
    pallas_call x1, Pallas kernels, body(): pl.pallas_call(lambda *refs: tables_kernel(*refs, bands=bands, subs=subs,...  4.76 us
    pallas_call x1, Pallas kernels, body(): pl.pallas_call(lambda *refs: middle_kernel(*refs, subs=subs, per=per, con...  4.41 us
    all_to_all x1, starting transfers between devices, exchanged(): return lax.all_to_all(x, axes, 0, 0, tiled=True)  3.65 us
    pallas_call x1, Pallas kernels, body(): pl.pallas_call(lambda *refs: backward_kernel(*refs, cols=cols), out_shape...  3.05 us
  transfers between devices with their start and end apart: 2, of which 2 were waited for; matrix products, arithmetic and copies ran while one was open for 0% of the time, Pallas kernels for 4%

profile of v1, /device:TPU:1, one launch (start us, length us, event | category | flops | bytes accessed | tf_op | source)
XLA Modules:
  0.0 106.7 jit_solution(16835099459267980186)
XLA Ops:
  0.7 0.0 copy-start.1
  0.7 0.7 copy-done.1
  1.4 0.7 copy-done.3
  2.0 0.7 copy-done.5
  2.7 5.0 %forward.1 = bf16[2,4,256,256]{3,2,1,0:T(8,128)(2,1)S(1)} custom-call(s32[1]{0:T(128)} %bitcast.refs_0_, s32[2,64]{1,0:T(2,128)S(1)} %bitcast.14, s32[8]{0:T(128)S(1)} %copy-done.5, s32[1]{0:T(128)S(6)} %copy.9.refs_3_, f32[1,2048]{1,0:T(1,128)S(1)} %bitcast.12, bf16[512,2048]{1,0:T(8,128)(2,1)} %refs_5_.1), custom_call_target="tpu_custom_call" | custom-call | tf_op jit(solution)/shard_map/forward/pallas_call | solution.py:240
  7.7 22.7 %all_to_all.20 = bf16[16,128,256]{2,1,0:T(8,128)(2,1)S(1)} all-to-all(bf16[16,128,256]{2,1,0:T(8,128)(2,1)S(1)} %bitcast.9), channel_id=1, replica_groups=mesh['y'=4,'zh'=4,'x'=4,'zl'=4,'core'=2] {'y','x'}, dimensions={0} | all-to-all | bytes 2097152 | tf_op jit(solution)/shard_map/all_to_all | solution.py:209
  30.4 0.1 reduce_sum.24.refs_5_
  30.6 0.0 copy-start
  30.6 0.0 copy-start.4
  30.6 0.0 copy-start.6
  30.6 27.1 %all_to_all.21 = bf16[16,8,256]{2,1,0:T(8,128)(2,1)S(1)} all-to-all(bf16[16,8,256]{2,1,0:T(8,128)(2,1)S(1)} %bitcast.11), channel_id=1, replica_groups=mesh['y'=4,'zh'=4,'x'=4,'zl'=4,'core'=2] {'zh','zl'}, dimensions={0} | all-to-all | bytes 131072 | tf_op jit(solution)/shard_map/all_to_all | solution.py:209
  57.8 14.4 %all_to_all.22 = bf16[16,8,256]{2,1,0:T(8,128)(2,1)S(1)} all-to-all(bf16[16,8,256]{2,1,0:T(8,128)(2,1)S(1)} %broadcast_in_dim.6), channel_id=1, replica_groups=mesh['y'=4,'zh'=4,'x'=4,'zl'=4,'core'=2] {'zh','zl'}, dimensions={0} | all-to-all | bytes 131072 | tf_op jit(solution)/shard_map/all_to_all | solution.py:209
  72.2 1.1 %broadcast_in_dim.7 = bf16[16,128,256]{2,1,0:T(8,128)(2,1)} broadcast(bf16[128,256]{1,0:T(8,128)(2,1)S(1)} %bitcast.16), dimensions={1,2} | broadcast | bytes 1114112 | tf_op jit(solution)/shard_map/broadcast_in_dim | solution.py:278
  73.2 3.7 %all-to-all-start.3 = ((bf16[16,128,256]{2,1,0:T(8,128)(2,1)}), bf16[16,128,256]{2,1,0:T(8,128)(2,1)S(1)}, u32[]{:S(2)}, u32[]{:S(2)}) async-start(bf16[16,128,256]{2,1,0:T(8,128)(2,1)} %broadcast_in_dim.7), calls=%async_computation.3 | async-start | bytes 2097152 | tf_op jit(solution)/shard_map/all_to_all | solution.py:209
  76.9 0.0 copy-done.7
  76.9 0.1 copy.8
  77.0 0.0 copy-done
  77.0 0.0 copy-done.4
  77.0 4.8 %tables.1 = (bf16[4,2,256,512]{3,2,1,0:T(8,128)(2,1)}, bf16[512,2048]{1,0:T(8,128)(2,1)S(1)}, bf16[256,256]{1,0:T(8,128)(2,1)S(1)}) custom-call(s32[1]{0:T(128)} %bitcast.refs_0_, s32[2,64]{1,0:T(2,128)S(1)} %bitcast.15, s32[8]{0:T(128)S(1)} %copy-done.6, s32[1]{0:T(128)S(6)} %copy.9.refs_3_, bf16[256,256]{1,0:T(8,128)(2,1)S(1)} %copy-done, ...), custom_call_target="tpu_custom_call" | custom-call | flops 6000000000 | bytes 4000000 | tf_op jit(solution)/shard_map/tables/pallas_call | solution.py:260
  81.8 8.5 %all-to-all-done.3 = bf16[16,128,256]{2,1,0:T(8,128)(2,1)S(1)} async-done(((bf16[16,128,256]{2,1,0:T(8,128)(2,1)}), bf16[16,128,256]{2,1,0:T(8,128)(2,1)S(1)}, u32[]{:S(2)}, u32[]{:S(2)}) %all-to-all-start.3) | async-done | bytes 1048608 | tf_op jit(solution)/shard_map/all_to_all | solution.py:209
  90.3 4.4 %middle.1.refs_0_ = bf16[512,512]{1,0:T(8,128)(2,1)S(1)} custom-call(s32[1]{0:T(128)} %bitcast.refs_0_, bf16[2,4,256,256]{3,2,1,0:T(8,128)(2,1)S(1)} %bitcast.10, bf16[4,2,256,512]{3,2,1,0:T(8,128)(2,1)} %get-tuple-element.8.refs_2_, bf16[256,256]{1,0:T(8,128)(2,1)S(1)} %copy-done, bf16[256,256]{1,0:T(8,128)(2,1)S(1)} %get-tuple-element.9.refs_4_, ...), custom_call_target="tpu_custom_call" | custom-call | tf_op jit(solution)/shard_map/middle/pallas_call | solution.py:282
  94.7 7.4 %collective-permute-start = (bf16[512,512]{1,0:T(8,128)(2,1)S(1)}, bf16[512,512]{1,0:T(8,128)(2,1)S(1)}, u32[]{:S(2)}, u32[]{:S(2)}) collective-permute-start(bf16[512,512]{1,0:T(8,128)(2,1)S(1)} %middle.1.refs_0_), channel_id=1, source_target_pairs={{0,1},{1,0},{2,3},{3,2},{4,5},{5,4},{6,7},{7,6},{8,9},{9,8},{10,11... | collective-permute-start | bytes 1572872 | tf_op jit(solution)/shard_map/ppermute | solution.py:298
  102.1 1.5 %collective-permute-done.refs_1_ = bf16[512,512]{1,0:T(8,128)(2,1)S(1)} collective-permute-done((bf16[512,512]{1,0:T(8,128)(2,1)S(1)}, bf16[512,512]{1,0:T(8,128)(2,1)S(1)}, u32[]{:S(2)}, u32[]{:S(2)}) %collective-permute-start) | collective-permute-done | bytes 524320 | tf_op jit(solution)/shard_map/ppermute | solution.py:298
  103.6 3.0 %backward.1 = bf16[512,2048]{1,0:T(8,128)(2,1)} custom-call(bf16[512,512]{1,0:T(8,128)(2,1)S(1)} %middle.1.refs_0_, bf16[512,512]{1,0:T(8,128)(2,1)S(1)} %collective-permute-done.refs_1_, bf16[512,2048]{1,0:T(8,128)(2,1)S(1)} %get-tuple-element.10.refs_2_, f32[1,2048]{1,0:T(1,128)S(1)} %bitcast.13), custom_call_target="tpu_custom_call" | custom-call | tf_op jit(solution)/shard_map/backward/pallas_call | solution.py:300
  (9 shorter events, 0.1 us)
Async XLA Ops:
  0.7 0.7 copy-start.1
  1.4 0.7 copy-start.3
  2.0 0.7 copy-start.5
  30.4 46.5 %copy-start.7 = (s32[8,16,16]{2,1,0:T(8,128)S(1)}, s32[8,16,16]{2,1,0:T(8,128)}, u32[]{:S(2)}) copy-start(s32[8,16,16]{2,1,0:T(8,128)} %param.13) | copy-start | bytes 24580
  30.6 46.4 %copy-start = (bf16[256,256]{1,0:T(8,128)(2,1)S(1)}, bf16[256,256]{1,0:T(8,128)(2,1)}, u32[]{:S(2)}) copy-start(bf16[256,256]{1,0:T(8,128)(2,1)} %refs_3_.3) | copy-start | bytes 393220
  30.6 46.4 %copy-start.4 = (s32[64,2]{0,1:T(2,128)S(1)}, s32[64,2]{0,1:T(2,128)}, u32[]{:S(2)}) copy-start(s32[64,2]{0,1:T(2,128)} %param.9) | copy-start | bytes 1540
  30.6 46.4 %copy-start.6 = (s32[8]{0:T(128)S(1)}, s32[8]{0:T(128)}, u32[]{:S(2)}) copy-start(s32[8]{0:T(128)} %refs_2_.3) | copy-start | bytes 100
  73.2 17.0 %all-to-all-start.3 = ((bf16[16,128,256]{2,1,0:T(8,128)(2,1)}), bf16[16,128,256]{2,1,0:T(8,128)(2,1)S(1)}, u32[]{:S(2)}, u32[]{:S(2)}) async-start(bf16[16,128,256]{2,1,0:T(8,128)(2,1)} %broadcast_in_dim.7), calls=%async_computation.3 | async-start | bytes 2097152 | tf_op jit(solution)/shard_map/all_to_all | solution.py:209
  81.8 21.8 %copy-start.2 = (f32[2048]{0:T(1024)S(1)}, f32[2048]{0:T(1024)}, u32[]{:S(2)}) copy-start(f32[2048]{0:T(1024)} %param.8) | copy-start | bytes 24580
  94.7 8.9 %collective-permute-start = (bf16[512,512]{1,0:T(8,128)(2,1)S(1)}, bf16[512,512]{1,0:T(8,128)(2,1)S(1)}, u32[]{:S(2)}, u32[]{:S(2)}) collective-permute-start(bf16[512,512]{1,0:T(8,128)(2,1)S(1)} %middle.1.refs_0_), channel_id=1, source_target_pairs={{0,1},{1,0},{2,3},{3,2},{4,5},{5,4},{6,7},{7,6},{8,9},{9,8},{10,11... | collective-permute-start | bytes 1572872 | tf_op jit(solution)/shard_map/ppermute | solution.py:298

commit v2 on v1

--- a/solution.py
+++ b/solution.py
@@ -93,15 +93,33 @@
     nx, ny = facet_scr.shape
     blocks = contrib // STEP
 
-    small, (big_c, big_s) = column_factors(oy, col_ref[0], blocks, ny)
-    taper = window_ref[...] * b_scale
-    small = (small[0] * taper, small[1] * taper)
-    for a in range(blocks):
-        c, s = turned(big_c, big_s, a, *small)
-        lo = a * STEP
-        b_scr[lo : lo + STEP, :] = c.astype(jnp.bfloat16)
-        b_scr[contrib + lo : contrib + lo + STEP, :] = (-s).astype(jnp.bfloat16)
+    width = min(256, ny)
+
+    def columns(at, carry):
+        lanes = pl.ds(pl.multiple_of(at * width, width), width)
+        small, big = column_factors(oy + at * width, col_ref[0], blocks, width)
+        taper = window_ref[:, lanes] * b_scale
+        small = (small[0] * taper, small[1] * taper)
+        for a in range(blocks):
+            c, s = turned(*big, a, *small)
+            lo = a * STEP
+            b_scr[lo : lo + STEP, lanes] = c.astype(jnp.bfloat16)
+            b_scr[contrib + lo : contrib + lo + STEP, lanes] = (-s).astype(jnp.bfloat16)
+        return carry
+
+    lax.fori_loop(0, ny // width, columns, 0)
     load.wait()
+
+    v = wrapped(ox + band_at * nx + iota((STEP, nx), 1))
+    small_c, small_s = unit_circle(iota((STEP, nx), 0), v)
+    small = (small_c * a_scale, small_s * a_scale)
+    for s_at in range(per):
+
+        def store(lo, c, s):
+            a_scr[s_at, 0, lo : lo + STEP, :] = c
+            a_scr[s_at, 1, lo : lo + STEP, :] = s
+
+        row_table(rows_ref[sub_at * per + s_at], v, small, blocks, store)
     t = nt(b_scr[...], facet_scr[...])
     tr = t[:contrib].astype(jnp.bfloat16)
     ti = t[contrib:].astype(jnp.bfloat16)
@@ -109,17 +127,6 @@
     t_scr[0, contrib:, :] = ti
     t_scr[1, :contrib, :] = -ti
     t_scr[1, contrib:, :] = tr
-
-    v = wrapped(ox + band_at * nx + iota((STEP, nx), 1))
-    small_c, small_s = unit_circle(iota((STEP, nx), 0), v)
-    small = (small_c * a_scale, small_s * a_scale)
-    for s_at in range(per):
-
-        def store(lo, c, s):
-            a_scr[s_at, 0, lo : lo + STEP, :] = c
-            a_scr[s_at, 1, lo : lo + STEP, :] = s
-
-        row_table(rows_ref[sub_at * per + s_at], v, small, blocks, store)
     for s_at in range(per):
         part = nt(t_scr[0], a_scr[s_at, 0]) + nt(t_scr[1], a_scr[s_at, 1])
         part_ref[0, s_at] = part[:contrib].astype(jnp.bfloat16)
@@ -191,18 +198,21 @@
     e_ref[...] = total.T.astype(jnp.bfloat16)
 
 
-def backward_kernel(mine_ref, other_ref, d_ref, window_ref, out_ref, e_scr, *, cols):
-    at = pl.program_id(0)
-
-    @pl.when(at == 0)
-    def _():
-        e_scr[...] = (
-            mine_ref[...].astype(jnp.float32) + other_ref[...].astype(jnp.float32)
-        ).astype(jnp.bfloat16)
-
-    here = pl.ds(pl.multiple_of(at * cols, cols), cols)
-    image = nn(e_scr[...], d_ref[:, here])
-    out_ref[...] = (window_ref[:, here] * image).astype(jnp.bfloat16)
+def backward_kernel(mine_ref, other_ref, d_ref, window_ref, out_hbm, out_scr, sems, *, chunks):
+    cols = out_scr.shape[1] // chunks
+    e = (mine_ref[...].astype(jnp.float32) + other_ref[...].astype(jnp.float32)).astype(jnp.bfloat16)
+    sends = []
+    for j in range(chunks):
+        here = slice(j * cols, (j + 1) * cols)
+        image = nn(e, d_ref[:, here])
+        out_scr[:, here] = (window_ref[:, here] * image).astype(jnp.bfloat16)
+        send = pltpu.make_async_copy(
+            out_scr.at[:, pl.ds(j * cols, cols)], out_hbm.at[:, pl.ds(j * cols, cols)], sems.at[j]
+        )
+        send.start()
+        sends.append(send)
+    for send in sends:
+        send.wait()
 
 
 def exchanged(x, axes):
@@ -211,6 +221,10 @@
 
 def summed(x):
     return jnp.sum(x.astype(jnp.float32), axis=0).astype(jnp.bfloat16)
+
+
+def distant(x):
+    return pltpu.with_memory_space_constraint(x, pltpu.HBM)
 
 
 def near(x):
@@ -253,7 +267,7 @@
         ],
         compiler_params=pltpu.CompilerParams(vmem_limit_bytes=28 * 2**20),
         name="forward",
-    )(here, offsets, row_offsets, column_offset, taper, pltpu.with_memory_space_constraint(facets, pltpu.HBM))
+    )(here, distant(offsets), distant(row_offsets), column_offset, distant(taper), distant(facets))
 
     lines = 2 * per * contrib
     mine = summed(exchanged(part.reshape(plane, lines // plane, contrib), PLANE))
@@ -293,17 +307,16 @@
         ],
         compiler_params=pltpu.CompilerParams(vmem_limit_bytes=28 * 2**20),
         name="middle",
-    )(here, near(grid), pltpu.with_memory_space_constraint(a_table, pltpu.HBM), kernel, near(kernel_t), counts)
+    )(here, near(grid), distant(a_table), kernel, near(kernel_t), counts)
 
     other = lax.ppermute(e_part, "core", [(i, (i + 1) % subs) for i in range(subs)])
-    cols = ny // 4
+    chunks = 4
     return pl.pallas_call(
-        lambda *refs: backward_kernel(*refs, cols=cols),
+        lambda *refs: backward_kernel(*refs, chunks=chunks),
         out_shape=jax.ShapeDtypeStruct((nx, ny), jnp.bfloat16),
-        grid=(ny // cols,),
         in_specs=[vmem, vmem, vmem, vmem],
-        out_specs=pl.BlockSpec((nx, cols), lambda i: (0, i)),
-        scratch_shapes=[pltpu.VMEM((nx, 2 * contrib), jnp.bfloat16)],
+        out_specs=far,
+        scratch_shapes=[pltpu.VMEM((nx, ny), jnp.bfloat16), pltpu.SemaphoreType.DMA((chunks,))],
         compiler_params=pltpu.CompilerParams(vmem_limit_bytes=28 * 2**20),
         name="backward",
     )(near(e_part), near(other), near(d_table), taper)

time: 107 us -> 104 us (0.972)
  local copies, waits for them, and re-layouts: 3.21 us -> 1.18 us
    unnamed x17 -> x11, local copies, waits for them, and re-layouts: 2.13 us -> 0.1 us
  transfers between devices with their start and end apart: 2 -> 2, of which waited for: 2 -> 2; matrix products, arithmetic and copies ran while one was open for 0% -> 0% of each run, Pallas kernels for 4% -> 5%
where the time goes in v2:
time: 104 us
  blocking collectives  64.2 us (62%)
  Pallas kernels  16.4 us (16%)
  starting transfers between devices  11.1 us (11%)
  waiting for transfers between devices  9.97 us (10%)
  local copies, waits for them, and re-layouts  1.18 us (1%)
    all_to_all x3, blocking collectives, exchanged(): return lax.all_to_all(x, axes, 0, 0, tiled=True)  64.2 us
    all_to_all x1, waiting for transfers between devices, exchanged(): return lax.all_to_all(x, axes, 0, 0, tiled=True)  8.45 us
    ppermute x1, starting transfers between devices, body(): lax.ppermute(e_part, 'core', [(i, (i + 1) % subs) for i in range(subs)])  7.41 us
    pallas_call x1, Pallas kernels, body(): pl.pallas_call(lambda *refs: forward_kernel(*refs, bands=bands, subs=subs...  5.13 us
    pallas_call x1, Pallas kernels, body(): pl.pallas_call(lambda *refs: tables_kernel(*refs, bands=bands, subs=subs,...  4.76 us
    pallas_call x1, Pallas kernels, body(): pl.pallas_call(lambda *refs: middle_kernel(*refs, subs=subs, per=per, con...  4.4 us
    all_to_all x1, starting transfers between devices, exchanged(): return lax.all_to_all(x, axes, 0, 0, tiled=True)  3.65 us
    pallas_call x1, Pallas kernels, body(): pl.pallas_call(lambda *refs: backward_kernel(*refs, chunks=chunks), out_s...  2.1 us
  transfers between devices with their start and end apart: 2, of which 2 were waited for; matrix products, arithmetic and copies ran while one was open for 0% of the time, Pallas kernels for 5%

profile of v2, /device:TPU:1, one launch (start us, length us, event | category | flops | bytes accessed | tf_op | source)
XLA Modules:
  0.0 103.8 jit_solution(7418545915164702324)
XLA Ops:
  0.7 5.1 %forward.1 = bf16[2,4,256,256]{3,2,1,0:T(8,128)(2,1)S(1)} custom-call(s32[1]{0:T(128)} %bitcast.refs_0_, s32[2,64]{1,0:T(2,128)} %bitcast.14, s32[8]{0:T(128)} %refs_2_.3, s32[1]{0:T(128)S(6)} %copy.9.refs_3_, f32[1,2048]{1,0:T(1,128)} %bitcast.12, bf16[512,2048]{1,0:T(8,128)(2,1)} %refs_5_.1), custom_call_target="tpu_custom_call" | custom-call | tf_op jit(solution)/shard_map/forward/pallas_call | solution.py:254
  5.8 22.7 %all_to_all.20 = bf16[16,128,256]{2,1,0:T(8,128)(2,1)S(1)} all-to-all(bf16[16,128,256]{2,1,0:T(8,128)(2,1)S(1)} %bitcast.9), channel_id=1, replica_groups=mesh['y'=4,'zh'=4,'x'=4,'zl'=4,'core'=2] {'y','x'}, dimensions={0} | all-to-all | bytes 2097152 | tf_op jit(solution)/shard_map/all_to_all | solution.py:219
  28.5 0.0 copy-start.4
  28.5 0.1 reduce_sum.24.refs_5_
  28.7 0.0 copy-start
  28.7 0.0 copy-start.2
  28.7 0.0 copy-start.3
  28.7 27.1 %all_to_all.21 = bf16[16,8,256]{2,1,0:T(8,128)(2,1)S(1)} all-to-all(bf16[16,8,256]{2,1,0:T(8,128)(2,1)S(1)} %bitcast.11), channel_id=1, replica_groups=mesh['y'=4,'zh'=4,'x'=4,'zl'=4,'core'=2] {'zh','zl'}, dimensions={0} | all-to-all | bytes 131072 | tf_op jit(solution)/shard_map/all_to_all | solution.py:219
  55.8 14.4 %all_to_all.22 = bf16[16,8,256]{2,1,0:T(8,128)(2,1)S(1)} all-to-all(bf16[16,8,256]{2,1,0:T(8,128)(2,1)S(1)} %broadcast_in_dim.6), channel_id=1, replica_groups=mesh['y'=4,'zh'=4,'x'=4,'zl'=4,'core'=2] {'zh','zl'}, dimensions={0} | all-to-all | bytes 131072 | tf_op jit(solution)/shard_map/all_to_all | solution.py:219
  70.2 1.1 %broadcast_in_dim.7 = bf16[16,128,256]{2,1,0:T(8,128)(2,1)} broadcast(bf16[128,256]{1,0:T(8,128)(2,1)S(1)} %bitcast.16), dimensions={1,2} | broadcast | bytes 1114112 | tf_op jit(solution)/shard_map/broadcast_in_dim | solution.py:292
  71.3 3.7 %all-to-all-start.3 = ((bf16[16,128,256]{2,1,0:T(8,128)(2,1)}), bf16[16,128,256]{2,1,0:T(8,128)(2,1)S(1)}, u32[]{:S(2)}, u32[]{:S(2)}) async-start(bf16[16,128,256]{2,1,0:T(8,128)(2,1)} %broadcast_in_dim.7), calls=%async_computation.3 | async-start | bytes 2097152 | tf_op jit(solution)/shard_map/all_to_all | solution.py:219
  75.0 0.0 copy-done.4
  75.0 0.1 copy.8
  75.1 0.0 copy-done
  75.1 0.0 copy-done.2
  75.1 0.0 copy-done.3
  75.1 4.8 %tables.1 = (bf16[4,2,256,512]{3,2,1,0:T(8,128)(2,1)}, bf16[512,2048]{1,0:T(8,128)(2,1)S(1)}, bf16[256,256]{1,0:T(8,128)(2,1)S(1)}) custom-call(s32[1]{0:T(128)} %bitcast.refs_0_, s32[2,64]{1,0:T(2,128)S(1)} %bitcast.15, s32[8]{0:T(128)S(1)} %copy-done.3, s32[1]{0:T(128)S(6)} %copy.9.refs_3_, bf16[256,256]{1,0:T(8,128)(2,1)S(1)} %copy-done, ...), custom_call_target="tpu_custom_call" | custom-call | flops 6000000000 | bytes 4000000 | tf_op jit(solution)/shard_map/tables/pallas_call | solution.py:274
  79.9 0.0 copy-start.1
  79.9 8.5 %all-to-all-done.3 = bf16[16,128,256]{2,1,0:T(8,128)(2,1)S(1)} async-done(((bf16[16,128,256]{2,1,0:T(8,128)(2,1)}), bf16[16,128,256]{2,1,0:T(8,128)(2,1)S(1)}, u32[]{:S(2)}, u32[]{:S(2)}) %all-to-all-start.3) | async-done | bytes 1048608 | tf_op jit(solution)/shard_map/all_to_all | solution.py:219
  88.3 4.4 %middle.1.refs_0_ = bf16[512,512]{1,0:T(8,128)(2,1)S(1)} custom-call(s32[1]{0:T(128)} %bitcast.refs_0_, bf16[2,4,256,256]{3,2,1,0:T(8,128)(2,1)S(1)} %bitcast.10, bf16[4,2,256,512]{3,2,1,0:T(8,128)(2,1)} %get-tuple-element.8.refs_2_, bf16[256,256]{1,0:T(8,128)(2,1)S(1)} %copy-done, bf16[256,256]{1,0:T(8,128)(2,1)S(1)} %get-tuple-element.9.refs_4_, ...), custom_call_target="tpu_custom_call" | custom-call | tf_op jit(solution)/shard_map/middle/pallas_call | solution.py:296
  92.7 7.4 %collective-permute-start = (bf16[512,512]{1,0:T(8,128)(2,1)S(1)}, bf16[512,512]{1,0:T(8,128)(2,1)S(1)}, u32[]{:S(2)}, u32[]{:S(2)}) collective-permute-start(bf16[512,512]{1,0:T(8,128)(2,1)S(1)} %middle.1.refs_0_), channel_id=1, source_target_pairs={{0,1},{1,0},{2,3},{3,2},{4,5},{5,4},{6,7},{7,6},{8,9},{9,8},{10,11... | collective-permute-start | bytes 1572872 | tf_op jit(solution)/shard_map/ppermute | solution.py:312
  100.2 1.5 %collective-permute-done.refs_1_ = bf16[512,512]{1,0:T(8,128)(2,1)S(1)} collective-permute-done((bf16[512,512]{1,0:T(8,128)(2,1)S(1)}, bf16[512,512]{1,0:T(8,128)(2,1)S(1)}, u32[]{:S(2)}, u32[]{:S(2)}) %collective-permute-start) | collective-permute-done | bytes 524320 | tf_op jit(solution)/shard_map/ppermute | solution.py:312
  101.7 0.0 copy-done.1
  101.7 2.1 %backward.1 = bf16[512,2048]{1,0:T(8,128)(2,1)} custom-call(bf16[512,512]{1,0:T(8,128)(2,1)S(1)} %middle.1.refs_0_, bf16[512,512]{1,0:T(8,128)(2,1)S(1)} %collective-permute-done.refs_1_, bf16[512,2048]{1,0:T(8,128)(2,1)S(1)} %get-tuple-element.10.refs_2_, f32[1,2048]{1,0:T(1,128)S(1)} %bitcast.13), custom_call_target="tpu_custom_call" | custom-call | tf_op jit(solution)/shard_map/backward/pallas_call | solution.py:314
  (3 shorter events, 0.0 us)
Async XLA Ops:
  28.5 46.5 %copy-start.4 = (s32[8,16,16]{2,1,0:T(8,128)S(1)}, s32[8,16,16]{2,1,0:T(8,128)}, u32[]{:S(2)}) copy-start(s32[8,16,16]{2,1,0:T(8,128)} %param.13) | copy-start | bytes 24580
  28.7 46.4 %copy-start = (bf16[256,256]{1,0:T(8,128)(2,1)S(1)}, bf16[256,256]{1,0:T(8,128)(2,1)}, u32[]{:S(2)}) copy-start(bf16[256,256]{1,0:T(8,128)(2,1)} %refs_3_.3) | copy-start | bytes 393220
  28.7 46.4 %copy-start.2 = (s32[64,2]{0,1:T(2,128)S(1)}, s32[64,2]{0,1:T(2,128)}, u32[]{:S(2)}) copy-start(s32[64,2]{0,1:T(2,128)} %param.9) | copy-start | bytes 1540
  28.7 46.4 %copy-start.3 = (s32[8]{0:T(128)S(1)}, s32[8]{0:T(128)}, u32[]{:S(2)}) copy-start(s32[8]{0:T(128)} %refs_2_.3) | copy-start | bytes 100
  71.3 17.0 %all-to-all-start.3 = ((bf16[16,128,256]{2,1,0:T(8,128)(2,1)}), bf16[16,128,256]{2,1,0:T(8,128)(2,1)S(1)}, u32[]{:S(2)}, u32[]{:S(2)}) async-start(bf16[16,128,256]{2,1,0:T(8,128)(2,1)} %broadcast_in_dim.7), calls=%async_computation.3 | async-start | bytes 2097152 | tf_op jit(solution)/shard_map/all_to_all | solution.py:219
  79.9 21.8 %copy-start.1 = (f32[2048]{0:T(1024)S(1)}, f32[2048]{0:T(1024)}, u32[]{:S(2)}) copy-start(f32[2048]{0:T(1024)} %param.8) | copy-start | bytes 24580
  92.7 8.9 %collective-permute-start = (bf16[512,512]{1,0:T(8,128)(2,1)S(1)}, bf16[512,512]{1,0:T(8,128)(2,1)S(1)}, u32[]{:S(2)}, u32[]{:S(2)}) collective-permute-start(bf16[512,512]{1,0:T(8,128)(2,1)S(1)} %middle.1.refs_0_), channel_id=1, source_target_pairs={{0,1},{1,0},{2,3},{3,2},{4,5},{5,4},{6,7},{7,6},{8,9},{9,8},{10,11... | collective-permute-start | bytes 1572872 | tf_op jit(solution)/shard_map/ppermute | solution.py:312

commit v3 on v2

--- a/solution.py
+++ b/solution.py
@@ -81,7 +81,7 @@
 
 
 def forward_kernel(
-    where_ref, offs_ref, rows_ref, col_ref, window_ref, facet_hbm,
+    where_ref, offs_ref, rows_ref, col_ref, window_ref, kern_ref, facet_hbm,
     part_ref, facet_scr, b_scr, t_scr, a_scr, sem,
     *, bands, subs, per, contrib, a_scale, b_scale,
 ):
@@ -121,8 +121,9 @@
 
         row_table(rows_ref[sub_at * per + s_at], v, small, blocks, store)
     t = nt(b_scr[...], facet_scr[...])
-    tr = t[:contrib].astype(jnp.bfloat16)
-    ti = t[contrib:].astype(jnp.bfloat16)
+    k = kern_ref[...]
+    tr = nn(k, t[:contrib].astype(jnp.bfloat16)).astype(jnp.bfloat16)
+    ti = nn(k, t[contrib:].astype(jnp.bfloat16)).astype(jnp.bfloat16)
     t_scr[0, :contrib, :] = tr
     t_scr[0, contrib:, :] = ti
     t_scr[1, :contrib, :] = -ti
@@ -134,7 +135,7 @@
 
 
 def tables_kernel(
-    where_ref, offs_ref, rows_ref, col_ref, kern_ref, after_ref, a_ref, d_ref, kern_t_ref,
+    where_ref, offs_ref, rows_ref, col_ref, kern_ref, after_ref, a_ref, d_ref, a_scr, d_scr,
     *, bands, subs, per, contrib, a_scale, d_scale,
 ):
     del after_ref
@@ -143,57 +144,63 @@
     oy = offs_ref[1, facet_at]
     nx, ny = a_ref.shape[3], d_ref.shape[1]
     blocks = contrib // STEP
-    kern_t_ref[...] = kern_ref[...].astype(jnp.float32).T.astype(jnp.bfloat16)
-    small, (big_c, big_s) = column_factors(oy, col_ref[0], blocks, ny)
-    small = (small[0] * d_scale, small[1] * d_scale)
-    for a in range(blocks):
-        c, s = turned(big_c, big_s, a, *small)
-        lo = a * STEP
-        d_ref[lo : lo + STEP, :] = c.astype(jnp.bfloat16)
-        d_ref[contrib + lo : contrib + lo + STEP, :] = (-s).astype(jnp.bfloat16)
+    k = kern_ref[...]
     v = wrapped(ox + band_at * nx + iota((STEP, nx), 1))
     small_c, small_s = unit_circle(iota((STEP, nx), 0), v)
     small = (small_c * a_scale, small_s * a_scale)
     for s_at in range(per):
 
         def store(lo, c, s):
-            a_ref[s_at, 0, lo : lo + STEP, :] = c
-            a_ref[s_at, 1, lo : lo + STEP, :] = s
+            a_scr[s_at % 2, 0, lo : lo + STEP, :] = c
+            a_scr[s_at % 2, 1, lo : lo + STEP, :] = s
 
         row_table(rows_ref[sub_at * per + s_at], v, small, blocks, store)
+        for c_at in range(2):
+            a_ref[s_at, c_at] = nn(k, a_scr[s_at % 2, c_at]).astype(jnp.bfloat16)
+    width = min(256, ny)
+
+    def columns(at, carry):
+        lanes = pl.ds(pl.multiple_of(at * width, width), width)
+        small, big = column_factors(oy + at * width, col_ref[0], blocks, width)
+        small = (small[0] * d_scale, small[1] * d_scale)
+        for a in range(blocks):
+            c, s = turned(*big, a, *small)
+            lo = a * STEP
+            d_scr[0, lo : lo + STEP, :] = c.astype(jnp.bfloat16)
+            d_scr[1, lo : lo + STEP, :] = (-s).astype(jnp.bfloat16)
+        d_ref[:contrib, lanes] = nn(k, d_scr[0]).astype(jnp.bfloat16)
+        d_ref[contrib:, lanes] = nn(k, d_scr[1]).astype(jnp.bfloat16)
+        return carry
+
+    lax.fori_loop(0, ny // width, columns, 0)
 
 
 def middle_kernel(
-    where_ref, grid_ref, a_hbm, kern_ref, kern_t_ref, counts_ref, e_ref,
-    a_ref, y_scr, w_scr, r_scr, sem, *, subs, per, contrib, tile,
+    where_ref, lines_ref, a_hbm, kern_ref, counts_ref, e_ref, a_scr, w_scr, sems,
+    *, subs, per, contrib, tile,
 ):
-    load = pltpu.make_async_copy(a_hbm, a_ref, sem)
-    load.start()
+    loads = [pltpu.make_async_copy(a_hbm.at[s], a_scr.at[s], sems.at[s]) for s in range(per)]
+    for load in loads:
+        load.start()
     sub_at = where_ref[0] % subs
     tiles = contrib // tile
     k = kern_ref[...]
-    kt = kern_t_ref[...]
     spread = (iota((tiles, contrib), 1) // tile == iota((tiles, contrib), 0)).astype(jnp.bfloat16)
-    for c in range(2):
-        for s in range(per):
-            y_scr[c, s] = nn(k, grid_ref[c, s]).astype(jnp.bfloat16)
     for s in range(per):
         count = nn(counts_ref[sub_at * per + s], spread)
         weight = (count / (count + 4.0))[:, None, :]
-        for c in range(2):
-            z = nt(y_scr[c, s], k).reshape(tiles, tile, contrib)
-            w_scr[c, s] = (weight * z).reshape(contrib, contrib).astype(jnp.bfloat16)
-    for s in range(per):
-        for c in range(2):
-            u = nn(w_scr[c, s], k).astype(jnp.bfloat16)
-            r_scr[s, c] = nn(kt, u).astype(jnp.bfloat16)
-    load.wait()
+        wr, wi = (
+            (weight * nt(lines_ref[c, s], k).reshape(tiles, tile, contrib)).reshape(contrib, contrib)
+            for c in range(2)
+        )
+        w_scr[s, 0, :contrib, :] = wr.astype(jnp.bfloat16)
+        w_scr[s, 0, contrib:, :] = wi.astype(jnp.bfloat16)
+        w_scr[s, 1, :contrib, :] = wi.astype(jnp.bfloat16)
+        w_scr[s, 1, contrib:, :] = (-wr).astype(jnp.bfloat16)
     total = None
     for s in range(per):
-        rr = r_scr[s, 0]
-        ri = r_scr[s, 1]
-        here = nn(jnp.concatenate([rr, ri], 0), a_ref[s, 0])
-        here = here + nn(jnp.concatenate([ri, -rr], 0), a_ref[s, 1])
+        loads[s].wait()
+        here = nn(w_scr[s, 0], a_scr[s, 0]) + nn(w_scr[s, 1], a_scr[s, 1])
         total = here if total is None else total + here
     e_ref[...] = total.T.astype(jnp.bfloat16)
 
@@ -256,7 +263,7 @@
             *refs, bands=bands, subs=subs, per=per, contrib=contrib, a_scale=a_scale, b_scale=b_scale,
         ),
         out_shape=pltpu.VMEM((2, per, contrib, contrib), jnp.bfloat16),
-        in_specs=[smem, smem, smem, smem, vmem, far],
+        in_specs=[smem, smem, smem, smem, vmem, vmem, far],
         out_specs=vmem,
         scratch_shapes=[
             pltpu.VMEM((nx, ny), jnp.bfloat16),
@@ -267,21 +274,24 @@
         ],
         compiler_params=pltpu.CompilerParams(vmem_limit_bytes=28 * 2**20),
         name="forward",
-    )(here, distant(offsets), distant(row_offsets), column_offset, distant(taper), distant(facets))
+    )(here, distant(offsets), distant(row_offsets), column_offset, distant(taper), distant(kernel), distant(facets))
 
     lines = 2 * per * contrib
     mine = summed(exchanged(part.reshape(plane, lines // plane, contrib), PLANE))
-    a_table, d_table, kernel_t = pl.pallas_call(
+    a_table, d_table = pl.pallas_call(
         lambda *refs: tables_kernel(
             *refs, bands=bands, subs=subs, per=per, contrib=contrib, a_scale=a_scale, d_scale=d_scale,
         ),
         out_shape=(
             pltpu.HBM((per, 2, contrib, nx), jnp.bfloat16),
             pltpu.VMEM((2 * contrib, ny), jnp.bfloat16),
-            pltpu.VMEM((contrib, contrib), jnp.bfloat16),
         ),
         in_specs=[smem, smem, smem, smem, vmem, anywhere],
-        out_specs=(vmem, vmem, vmem),
+        out_specs=(vmem, vmem),
+        scratch_shapes=[
+            pltpu.VMEM((2, 2, contrib, nx), jnp.bfloat16),
+            pltpu.VMEM((2, contrib, min(256, ny)), jnp.bfloat16),
+        ],
         cost_estimate=pl.CostEstimate(flops=6_000_000_000, transcendentals=0, bytes_accessed=4_000_000),
         compiler_params=pltpu.CompilerParams(vmem_limit_bytes=20 * 2**20),
         name="tables",
@@ -296,18 +306,16 @@
     e_part = pl.pallas_call(
         lambda *refs: middle_kernel(*refs, subs=subs, per=per, contrib=contrib, tile=tile),
         out_shape=pltpu.VMEM((nx, 2 * contrib), jnp.bfloat16),
-        in_specs=[smem, vmem, far, vmem, vmem, vmem],
+        in_specs=[smem, vmem, far, vmem, vmem],
         out_specs=vmem,
         scratch_shapes=[
             pltpu.VMEM((per, 2, contrib, nx), jnp.bfloat16),
-            pltpu.VMEM((2, per, contrib, contrib), jnp.bfloat16),
-            pltpu.VMEM((2, per, contrib, contrib), jnp.bfloat16),
-            pltpu.VMEM((per, 2, contrib, contrib), jnp.bfloat16),
-            pltpu.SemaphoreType.DMA(()),
+            pltpu.VMEM((per, 2, 2 * contrib, contrib), jnp.bfloat16),
+            pltpu.SemaphoreType.DMA((per,)),
         ],
         compiler_params=pltpu.CompilerParams(vmem_limit_bytes=28 * 2**20),
         name="middle",
-    )(here, near(grid), distant(a_table), kernel, near(kernel_t), counts)
+    )(here, near(grid), distant(a_table), kernel, counts)
 
     other = lax.ppermute(e_part, "core", [(i, (i + 1) % subs) for i in range(subs)])
     chunks = 4

time: 104 us -> 103 us (level)
  waiting for transfers between devices: 9.97 us -> 8.81 us
    pallas_call x1, Pallas kernels: 4.4 us -> 3.02 us  [body(): pl.pallas_call(lambda *refs: middle_kernel(*refs, subs=subs, per=per, con...]
    all_to_all x1, waiting for transfers between devices: 8.45 us -> 7.3 us  [exchanged(): return lax.all_to_all(x, axes, 0, 0, tiled=True)]
    pallas_call x1, Pallas kernels: 4.76 us -> 5.91 us  [body(): pl.pallas_call(lambda *refs: tables_kernel(*refs, bands=bands, subs=subs,...]
  transfers between devices with their start and end apart: 2 -> 2, of which waited for: 2 -> 2; matrix products, arithmetic and copies ran while one was open for 0% -> 0% of each run, Pallas kernels for 5% -> 6%
where the time goes in v3:
time: 103 us
  blocking collectives  64.2 us (62%)
  Pallas kernels  16.7 us (16%)
  starting transfers between devices  11.1 us (11%)
  waiting for transfers between devices  8.81 us (9%)
  local copies, waits for them, and re-layouts  1.18 us (1%)
    all_to_all x3, blocking collectives, exchanged(): return lax.all_to_all(x, axes, 0, 0, tiled=True)  64.2 us
    ppermute x1, starting transfers between devices, body(): lax.ppermute(e_part, 'core', [(i, (i + 1) % subs) for i in range(subs)])  7.41 us
    all_to_all x1, waiting for transfers between devices, exchanged(): return lax.all_to_all(x, axes, 0, 0, tiled=True)  7.3 us
    pallas_call x1, Pallas kernels, body(): pl.pallas_call(lambda *refs: tables_kernel(*refs, bands=bands, subs=subs,...  5.91 us
    pallas_call x1, Pallas kernels, body(): pl.pallas_call(lambda *refs: forward_kernel(*refs, bands=bands, subs=subs...  5.68 us
    all_to_all x1, starting transfers between devices, exchanged(): return lax.all_to_all(x, axes, 0, 0, tiled=True)  3.65 us
    pallas_call x1, Pallas kernels, body(): pl.pallas_call(lambda *refs: middle_kernel(*refs, subs=subs, per=per, con...  3.02 us
    pallas_call x1, Pallas kernels, body(): pl.pallas_call(lambda *refs: backward_kernel(*refs, chunks=chunks), out_s...  2.1 us
  transfers between devices with their start and end apart: 2, of which 2 were waited for; matrix products, arithmetic and copies ran while one was open for 0% of the time, Pallas kernels for 6%

profile of v3, /device:TPU:1, one launch (start us, length us, event | category | flops | bytes accessed | tf_op | source)
XLA Modules:
  0.0 102.9 jit_solution(7089181176072146452)
XLA Ops:
  0.7 5.7 %forward.1 = bf16[2,4,256,256]{3,2,1,0:T(8,128)(2,1)S(1)} custom-call(s32[1]{0:T(128)} %bitcast.refs_0_, s32[2,64]{1,0:T(2,128)} %bitcast.14, s32[8]{0:T(128)} %refs_2_.3, s32[1]{0:T(128)S(6)} %copy.9.refs_3_, f32[1,2048]{1,0:T(1,128)} %bitcast.12, bf16[256,256]{1,0:T(8,128)(2,1)} %refs_3_.3, bf16[512,2048]{1,0:T(8,128)(2,1)} %refs_6_.1), custom_call_target="tpu_custom_call" | custom-call | tf_op jit(solution)/shard_map/forward/pallas_call | solution.py:261
  6.3 22.7 %all_to_all.20 = bf16[16,128,256]{2,1,0:T(8,128)(2,1)S(1)} all-to-all(bf16[16,128,256]{2,1,0:T(8,128)(2,1)S(1)} %bitcast.9), channel_id=1, replica_groups=mesh['y'=4,'zh'=4,'x'=4,'zl'=4,'core'=2] {'y','x'}, dimensions={0} | all-to-all | bytes 2097152 | tf_op jit(solution)/shard_map/all_to_all | solution.py:226
  29.1 0.0 copy-start.4
  29.1 0.1 reduce_sum.24.refs_5_
  29.2 0.0 copy-start
  29.2 0.0 copy-start.2
  29.2 0.0 copy-start.3
  29.2 27.1 %all_to_all.21 = bf16[16,8,256]{2,1,0:T(8,128)(2,1)S(1)} all-to-all(bf16[16,8,256]{2,1,0:T(8,128)(2,1)S(1)} %bitcast.11), channel_id=1, replica_groups=mesh['y'=4,'zh'=4,'x'=4,'zl'=4,'core'=2] {'zh','zl'}, dimensions={0} | all-to-all | bytes 131072 | tf_op jit(solution)/shard_map/all_to_all | solution.py:226
  56.4 14.4 %all_to_all.22 = bf16[16,8,256]{2,1,0:T(8,128)(2,1)S(1)} all-to-all(bf16[16,8,256]{2,1,0:T(8,128)(2,1)S(1)} %broadcast_in_dim.6), channel_id=1, replica_groups=mesh['y'=4,'zh'=4,'x'=4,'zl'=4,'core'=2] {'zh','zl'}, dimensions={0} | all-to-all | bytes 131072 | tf_op jit(solution)/shard_map/all_to_all | solution.py:226
  70.8 1.1 %broadcast_in_dim.7 = bf16[16,128,256]{2,1,0:T(8,128)(2,1)} broadcast(bf16[128,256]{1,0:T(8,128)(2,1)S(1)} %bitcast.16), dimensions={1,2} | broadcast | bytes 1114112 | tf_op jit(solution)/shard_map/broadcast_in_dim | solution.py:302
  71.9 3.7 %all-to-all-start.3 = ((bf16[16,128,256]{2,1,0:T(8,128)(2,1)}), bf16[16,128,256]{2,1,0:T(8,128)(2,1)S(1)}, u32[]{:S(2)}, u32[]{:S(2)}) async-start(bf16[16,128,256]{2,1,0:T(8,128)(2,1)} %broadcast_in_dim.7), calls=%async_computation.3 | async-start | bytes 2097152 | tf_op jit(solution)/shard_map/all_to_all | solution.py:226
  75.5 0.0 copy-done.4
  75.5 0.1 copy.8
  75.6 0.0 copy-done
  75.6 0.0 copy-done.2
  75.7 0.0 copy-done.3
  75.7 5.9 %tables.1 = (bf16[4,2,256,512]{3,2,1,0:T(8,128)(2,1)}, bf16[512,2048]{1,0:T(8,128)(2,1)S(1)}) custom-call(s32[1]{0:T(128)} %bitcast.refs_0_, s32[2,64]{1,0:T(2,128)S(1)} %bitcast.15, s32[8]{0:T(128)S(1)} %copy-done.3, s32[1]{0:T(128)S(6)} %copy.9.refs_3_, bf16[256,256]{1,0:T(8,128)(2,1)S(1)} %copy-done, bf16[128,256]{1,0:T(8,128)(2,1)S(1)} %reduce_sum.24.refs_5_), custom_call_target="tpu_custom_call" | custom-call | flops 6000000000 | bytes 4000000 | tf_op jit(solution)/shard_map/tables/pallas_call | solution.py:281
  81.6 0.0 copy-start.1
  81.6 7.3 %all-to-all-done.3 = bf16[16,128,256]{2,1,0:T(8,128)(2,1)S(1)} async-done(((bf16[16,128,256]{2,1,0:T(8,128)(2,1)}), bf16[16,128,256]{2,1,0:T(8,128)(2,1)S(1)}, u32[]{:S(2)}, u32[]{:S(2)}) %all-to-all-start.3) | async-done | bytes 1048608 | tf_op jit(solution)/shard_map/all_to_all | solution.py:226
  88.9 3.0 %middle.1.refs_0_ = bf16[512,512]{1,0:T(8,128)(2,1)S(1)} custom-call(s32[1]{0:T(128)} %bitcast.refs_0_, bf16[2,4,256,256]{3,2,1,0:T(8,128)(2,1)S(1)} %bitcast.10, bf16[4,2,256,512]{3,2,1,0:T(8,128)(2,1)} %get-tuple-element.7.refs_2_, bf16[256,256]{1,0:T(8,128)(2,1)S(1)} %copy-done, bf16[8,16,16]{2,1,0:T(8,128)(2,1)S(1)} %convert_bitcast_fusion.refs_4_), custom_call_target="tpu_custom_call" | custom-call | tf_op jit(solution)/shard_map/middle/pallas_call | solution.py:306
  91.9 7.4 %collective-permute-start = (bf16[512,512]{1,0:T(8,128)(2,1)S(1)}, bf16[512,512]{1,0:T(8,128)(2,1)S(1)}, u32[]{:S(2)}, u32[]{:S(2)}) collective-permute-start(bf16[512,512]{1,0:T(8,128)(2,1)S(1)} %middle.1.refs_0_), channel_id=1, source_target_pairs={{0,1},{1,0},{2,3},{3,2},{4,5},{5,4},{6,7},{7,6},{8,9},{9,8},{10,11... | collective-permute-start | bytes 1572872 | tf_op jit(solution)/shard_map/ppermute | solution.py:320
  99.3 1.5 %collective-permute-done.refs_1_ = bf16[512,512]{1,0:T(8,128)(2,1)S(1)} collective-permute-done((bf16[512,512]{1,0:T(8,128)(2,1)S(1)}, bf16[512,512]{1,0:T(8,128)(2,1)S(1)}, u32[]{:S(2)}, u32[]{:S(2)}) %collective-permute-start) | collective-permute-done | bytes 524320 | tf_op jit(solution)/shard_map/ppermute | solution.py:320
  100.8 0.0 copy-done.1
  100.9 2.1 %backward.1 = bf16[512,2048]{1,0:T(8,128)(2,1)} custom-call(bf16[512,512]{1,0:T(8,128)(2,1)S(1)} %middle.1.refs_0_, bf16[512,512]{1,0:T(8,128)(2,1)S(1)} %collective-permute-done.refs_1_, bf16[512,2048]{1,0:T(8,128)(2,1)S(1)} %get-tuple-element.8.refs_2_, f32[1,2048]{1,0:T(1,128)S(1)} %bitcast.13), custom_call_target="tpu_custom_call" | custom-call | tf_op jit(solution)/shard_map/backward/pallas_call | solution.py:322
  (3 shorter events, 0.0 us)
Async XLA Ops:
  29.1 46.5 %copy-start.4 = (s32[8,16,16]{2,1,0:T(8,128)S(1)}, s32[8,16,16]{2,1,0:T(8,128)}, u32[]{:S(2)}) copy-start(s32[8,16,16]{2,1,0:T(8,128)} %param.13) | copy-start | bytes 24580
  29.2 46.4 %copy-start = (bf16[256,256]{1,0:T(8,128)(2,1)S(1)}, bf16[256,256]{1,0:T(8,128)(2,1)}, u32[]{:S(2)}) copy-start(bf16[256,256]{1,0:T(8,128)(2,1)} %refs_3_.3) | copy-start | bytes 393220
  29.2 46.4 %copy-start.2 = (s32[64,2]{0,1:T(2,128)S(1)}, s32[64,2]{0,1:T(2,128)}, u32[]{:S(2)}) copy-start(s32[64,2]{0,1:T(2,128)} %param.9) | copy-start | bytes 1540
  29.2 46.4 %copy-start.3 = (s32[8]{0:T(128)S(1)}, s32[8]{0:T(128)}, u32[]{:S(2)}) copy-start(s32[8]{0:T(128)} %refs_2_.3) | copy-start | bytes 100
  71.9 17.0 %all-to-all-start.3 = ((bf16[16,128,256]{2,1,0:T(8,128)(2,1)}), bf16[16,128,256]{2,1,0:T(8,128)(2,1)S(1)}, u32[]{:S(2)}, u32[]{:S(2)}) async-start(bf16[16,128,256]{2,1,0:T(8,128)(2,1)} %broadcast_in_dim.7), calls=%async_computation.3 | async-start | bytes 2097152 | tf_op jit(solution)/shard_map/all_to_all | solution.py:226
  81.6 19.3 %copy-start.1 = (f32[2048]{0:T(1024)S(1)}, f32[2048]{0:T(1024)}, u32[]{:S(2)}) copy-start(f32[2048]{0:T(1024)} %param.8) | copy-start | bytes 24580
  91.9 8.9 %collective-permute-start = (bf16[512,512]{1,0:T(8,128)(2,1)S(1)}, bf16[512,512]{1,0:T(8,128)(2,1)S(1)}, u32[]{:S(2)}, u32[]{:S(2)}) collective-permute-start(bf16[512,512]{1,0:T(8,128)(2,1)S(1)} %middle.1.refs_0_), channel_id=1, source_target_pairs={{0,1},{1,0},{2,3},{3,2},{4,5},{5,4},{6,7},{7,6},{8,9},{9,8},{10,11... | collective-permute-start | bytes 1572872 | tf_op jit(solution)/shard_map/ppermute | solution.py:320

commit v4 on v3

--- a/solution.py
+++ b/solution.py
@@ -81,12 +81,21 @@
 
 
 def forward_kernel(
-    where_ref, offs_ref, rows_ref, col_ref, window_ref, kern_ref, facet_hbm,
-    part_ref, facet_scr, b_scr, t_scr, a_scr, sem,
+    where_ref, col_ref, offs_hbm, rows_hbm, window_hbm, kern_hbm, facet_hbm,
+    part_ref, offs_ref, rows_ref, window_ref, kern_ref, facet_scr, b_scr, t_scr, a_scr, sems,
     *, bands, subs, per, contrib, a_scale, b_scale,
 ):
-    load = pltpu.make_async_copy(facet_hbm, facet_scr, sem)
-    load.start()
+    loads = [
+        pltpu.make_async_copy(source, target, sems.at[i])
+        for i, (source, target) in enumerate((
+            (offs_hbm, offs_ref), (rows_hbm, rows_ref), (window_hbm, window_ref),
+            (kern_hbm, kern_ref), (facet_hbm, facet_scr),
+        ))
+    ]
+    for load in loads:
+        load.start()
+    for load in loads[:3]:
+        load.wait()
     facet_at, band_at, sub_at = place(where_ref, bands, subs)
     ox = offs_ref[0, facet_at]
     oy = offs_ref[1, facet_at]
@@ -108,7 +117,8 @@
         return carry
 
     lax.fori_loop(0, ny // width, columns, 0)
-    load.wait()
+    for load in loads[3:]:
+        load.wait()
 
     v = wrapped(ox + band_at * nx + iota((STEP, nx), 1))
     small_c, small_s = unit_circle(iota((STEP, nx), 0), v)
@@ -263,18 +273,22 @@
             *refs, bands=bands, subs=subs, per=per, contrib=contrib, a_scale=a_scale, b_scale=b_scale,
         ),
         out_shape=pltpu.VMEM((2, per, contrib, contrib), jnp.bfloat16),
-        in_specs=[smem, smem, smem, smem, vmem, vmem, far],
+        in_specs=[smem, smem, far, far, far, far, far],
         out_specs=vmem,
         scratch_shapes=[
+            pltpu.SMEM(offsets.shape, jnp.int32),
+            pltpu.SMEM(row_offsets.shape, jnp.int32),
+            pltpu.VMEM(taper.shape, jnp.float32),
+            pltpu.VMEM(kernel.shape, jnp.bfloat16),
             pltpu.VMEM((nx, ny), jnp.bfloat16),
             pltpu.VMEM((2 * contrib, ny), jnp.bfloat16),
             pltpu.VMEM((2, 2 * contrib, nx), jnp.bfloat16),
             pltpu.VMEM((per, 2, contrib, nx), jnp.bfloat16),
-            pltpu.SemaphoreType.DMA(()),
+            pltpu.SemaphoreType.DMA((5,)),
         ],
         compiler_params=pltpu.CompilerParams(vmem_limit_bytes=28 * 2**20),
         name="forward",
-    )(here, distant(offsets), distant(row_offsets), column_offset, distant(taper), distant(kernel), distant(facets))
+    )(here, column_offset, distant(offsets), distant(row_offsets), distant(taper), distant(kernel), distant(facets))
 
     lines = 2 * per * contrib
     mine = summed(exchanged(part.reshape(plane, lines // plane, contrib), PLANE))
@@ -318,7 +332,7 @@
     )(here, near(grid), distant(a_table), kernel, counts)
 
     other = lax.ppermute(e_part, "core", [(i, (i + 1) % subs) for i in range(subs)])
-    chunks = 4
+    chunks = 8
     return pl.pallas_call(
         lambda *refs: backward_kernel(*refs, chunks=chunks),
         out_shape=jax.ShapeDtypeStruct((nx, ny), jnp.bfloat16),

time: 103 us -> 103 us (level)
  no operation moved by 1% of the time
where the time goes in v4:
time: 103 us; the launch traced here: 102 us
  blocking collectives  64.2 us (62%)
  Pallas kernels  16.2 us (16%)
  starting transfers between devices  11.1 us (11%)
  waiting for transfers between devices  8.81 us (9%)
  local copies, waits for them, and re-layouts  1.18 us (1%)
    all_to_all x3, blocking collectives, exchanged(): return lax.all_to_all(x, axes, 0, 0, tiled=True)  64.2 us
    ppermute x1, starting transfers between devices, body(): lax.ppermute(e_part, 'core', [(i, (i + 1) % subs) for i in range(subs)])  7.41 us
    all_to_all x1, waiting for transfers between devices, exchanged(): return lax.all_to_all(x, axes, 0, 0, tiled=True)  7.3 us
    pallas_call x1, Pallas kernels, body(): pl.pallas_call(lambda *refs: tables_kernel(*refs, bands=bands, subs=subs,...  5.92 us
    pallas_call x1, Pallas kernels, body(): pl.pallas_call(lambda *refs: forward_kernel(*refs, bands=bands, subs=subs...  5.04 us
    all_to_all x1, starting transfers between devices, exchanged(): return lax.all_to_all(x, axes, 0, 0, tiled=True)  3.65 us
    pallas_call x1, Pallas kernels, body(): pl.pallas_call(lambda *refs: middle_kernel(*refs, subs=subs, per=per, con...  3.02 us
    pallas_call x1, Pallas kernels, body(): pl.pallas_call(lambda *refs: backward_kernel(*refs, chunks=chunks), out_s...  2.27 us
  transfers between devices with their start and end apart: 2, of which 2 were waited for; matrix products, arithmetic and copies ran while one was open for 0% of the time, Pallas kernels for 6%

profile of v4, /device:TPU:1, one launch (start us, length us, event | category | flops | bytes accessed | tf_op | source)
XLA Modules:
  0.0 102.5 jit_solution(888684211023775327)
XLA Ops:
  0.7 5.0 %forward.1 = bf16[2,4,256,256]{3,2,1,0:T(8,128)(2,1)S(1)} custom-call(s32[1]{0:T(128)} %bitcast.refs_0_, s32[1]{0:T(128)S(6)} %copy.9.refs_1_.refs_3_, s32[2,64]{1,0:T(2,128)} %bitcast.14, s32[8]{0:T(128)} %refs_2_.1, f32[1,2048]{1,0:T(1,128)} %bitcast.12, bf16[256,256]{1,0:T(8,128)(2,1)} %refs_3_.4, bf16[512,2048]{1,0:T(8,128)(2,1)} %refs_6_.1), custom_call_target="tpu_custom_call" | custom-call | tf_op jit(solution)/shard_map/forward/pallas_call | solution.py:271
  5.7 22.7 %all_to_all.20 = bf16[16,128,256]{2,1,0:T(8,128)(2,1)S(1)} all-to-all(bf16[16,128,256]{2,1,0:T(8,128)(2,1)S(1)} %bitcast.9), channel_id=1, replica_groups=mesh['y'=4,'zh'=4,'x'=4,'zl'=4,'core'=2] {'y','x'}, dimensions={0} | all-to-all | bytes 2097152 | tf_op jit(solution)/shard_map/all_to_all | solution.py:236
  28.4 0.0 copy-start.4
  28.4 0.1 reduce_sum.24.refs_5_
  28.6 0.0 copy-start
  28.6 0.0 copy-start.2
  28.6 0.0 copy-start.3
  28.6 27.1 %all_to_all.21 = bf16[16,8,256]{2,1,0:T(8,128)(2,1)S(1)} all-to-all(bf16[16,8,256]{2,1,0:T(8,128)(2,1)S(1)} %bitcast.11), channel_id=1, replica_groups=mesh['y'=4,'zh'=4,'x'=4,'zl'=4,'core'=2] {'zh','zl'}, dimensions={0} | all-to-all | bytes 131072 | tf_op jit(solution)/shard_map/all_to_all | solution.py:236
  55.8 14.4 %all_to_all.22 = bf16[16,8,256]{2,1,0:T(8,128)(2,1)S(1)} all-to-all(bf16[16,8,256]{2,1,0:T(8,128)(2,1)S(1)} %broadcast_in_dim.6), channel_id=1, replica_groups=mesh['y'=4,'zh'=4,'x'=4,'zl'=4,'core'=2] {'zh','zl'}, dimensions={0} | all-to-all | bytes 131072 | tf_op jit(solution)/shard_map/all_to_all | solution.py:236
  70.2 1.1 %broadcast_in_dim.7 = bf16[16,128,256]{2,1,0:T(8,128)(2,1)} broadcast(bf16[128,256]{1,0:T(8,128)(2,1)S(1)} %bitcast.16), dimensions={1,2} | broadcast | bytes 1114112 | tf_op jit(solution)/shard_map/broadcast_in_dim | solution.py:316
  71.2 3.7 %all-to-all-start.3 = ((bf16[16,128,256]{2,1,0:T(8,128)(2,1)}), bf16[16,128,256]{2,1,0:T(8,128)(2,1)S(1)}, u32[]{:S(2)}, u32[]{:S(2)}) async-start(bf16[16,128,256]{2,1,0:T(8,128)(2,1)} %broadcast_in_dim.7), calls=%async_computation.3 | async-start | bytes 2097152 | tf_op jit(solution)/shard_map/all_to_all | solution.py:236
  74.9 0.0 copy-done.4
  74.9 0.1 copy.8
  75.0 0.0 copy-done
  75.0 0.0 copy-done.2
  75.0 0.0 copy-done.3
  75.0 5.9 %tables.1 = (bf16[4,2,256,512]{3,2,1,0:T(8,128)(2,1)}, bf16[512,2048]{1,0:T(8,128)(2,1)S(1)}) custom-call(s32[1]{0:T(128)} %bitcast.refs_0_, s32[2,64]{1,0:T(2,128)S(1)} %bitcast.15, s32[8]{0:T(128)S(1)} %copy-done.3, s32[1]{0:T(128)S(6)} %copy.9.refs_1_.refs_3_, bf16[256,256]{1,0:T(8,128)(2,1)S(1)} %copy-done, bf16[128,256]{1,0:T(8,128)(2,1)S(1)} %reduce_sum.24.refs_5_), custom_call_target="tpu_custom_call" | custom-call | flops 6000000000 | bytes 4000000 | tf_op jit(solution)/shard_map/tables/pallas_call | solution.py:295
  80.9 0.0 copy-start.1
  81.0 7.3 %all-to-all-done.3 = bf16[16,128,256]{2,1,0:T(8,128)(2,1)S(1)} async-done(((bf16[16,128,256]{2,1,0:T(8,128)(2,1)}), bf16[16,128,256]{2,1,0:T(8,128)(2,1)S(1)}, u32[]{:S(2)}, u32[]{:S(2)}) %all-to-all-start.3) | async-done | bytes 1048608 | tf_op jit(solution)/shard_map/all_to_all | solution.py:236
  88.2 3.0 %middle.1.refs_0_ = bf16[512,512]{1,0:T(8,128)(2,1)S(1)} custom-call(s32[1]{0:T(128)} %bitcast.refs_0_, bf16[2,4,256,256]{3,2,1,0:T(8,128)(2,1)S(1)} %bitcast.10, bf16[4,2,256,512]{3,2,1,0:T(8,128)(2,1)} %get-tuple-element.7.refs_2_, bf16[256,256]{1,0:T(8,128)(2,1)S(1)} %copy-done, bf16[8,16,16]{2,1,0:T(8,128)(2,1)S(1)} %convert_bitcast_fusion.refs_4_), custom_call_target="tpu_custom_call" | custom-call | tf_op jit(solution)/shard_map/middle/pallas_call | solution.py:320
  91.3 7.4 %collective-permute-start = (bf16[512,512]{1,0:T(8,128)(2,1)S(1)}, bf16[512,512]{1,0:T(8,128)(2,1)S(1)}, u32[]{:S(2)}, u32[]{:S(2)}) collective-permute-start(bf16[512,512]{1,0:T(8,128)(2,1)S(1)} %middle.1.refs_0_), channel_id=1, source_target_pairs={{0,1},{1,0},{2,3},{3,2},{4,5},{5,4},{6,7},{7,6},{8,9},{9,8},{10,11... | collective-permute-start | bytes 1572872 | tf_op jit(solution)/shard_map/ppermute | solution.py:334
  98.7 1.5 %collective-permute-done.refs_1_ = bf16[512,512]{1,0:T(8,128)(2,1)S(1)} collective-permute-done((bf16[512,512]{1,0:T(8,128)(2,1)S(1)}, bf16[512,512]{1,0:T(8,128)(2,1)S(1)}, u32[]{:S(2)}, u32[]{:S(2)}) %collective-permute-start) | collective-permute-done | bytes 524320 | tf_op jit(solution)/shard_map/ppermute | solution.py:334
  100.2 0.0 copy-done.1
  100.2 2.3 %backward.1 = bf16[512,2048]{1,0:T(8,128)(2,1)} custom-call(bf16[512,512]{1,0:T(8,128)(2,1)S(1)} %middle.1.refs_0_, bf16[512,512]{1,0:T(8,128)(2,1)S(1)} %collective-permute-done.refs_1_, bf16[512,2048]{1,0:T(8,128)(2,1)S(1)} %get-tuple-element.8.refs_2_, f32[1,2048]{1,0:T(1,128)S(1)} %bitcast.13), custom_call_target="tpu_custom_call" | custom-call | tf_op jit(solution)/shard_map/backward/pallas_call | solution.py:336
  (3 shorter events, 0.0 us)
Async XLA Ops:
  28.4 46.5 %copy-start.4 = (s32[8,16,16]{2,1,0:T(8,128)S(1)}, s32[8,16,16]{2,1,0:T(8,128)}, u32[]{:S(2)}) copy-start(s32[8,16,16]{2,1,0:T(8,128)} %param.13) | copy-start | bytes 24580
  28.6 46.4 %copy-start = (bf16[256,256]{1,0:T(8,128)(2,1)S(1)}, bf16[256,256]{1,0:T(8,128)(2,1)}, u32[]{:S(2)}) copy-start(bf16[256,256]{1,0:T(8,128)(2,1)} %refs_3_.4) | copy-start | bytes 393220
  28.6 46.4 %copy-start.2 = (s32[64,2]{0,1:T(2,128)S(1)}, s32[64,2]{0,1:T(2,128)}, u32[]{:S(2)}) copy-start(s32[64,2]{0,1:T(2,128)} %param.9) | copy-start | bytes 1540
  28.6 46.4 %copy-start.3 = (s32[8]{0:T(128)S(1)}, s32[8]{0:T(128)}, u32[]{:S(2)}) copy-start(s32[8]{0:T(128)} %refs_2_.1) | copy-start | bytes 100
  71.2 17.0 %all-to-all-start.3 = ((bf16[16,128,256]{2,1,0:T(8,128)(2,1)}), bf16[16,128,256]{2,1,0:T(8,128)(2,1)S(1)}, u32[]{:S(2)}, u32[]{:S(2)}) async-start(bf16[16,128,256]{2,1,0:T(8,128)(2,1)} %broadcast_in_dim.7), calls=%async_computation.3 | async-start | bytes 2097152 | tf_op jit(solution)/shard_map/all_to_all | solution.py:236
  80.9 19.3 %copy-start.1 = (f32[2048]{0:T(1024)S(1)}, f32[2048]{0:T(1024)}, u32[]{:S(2)}) copy-start(f32[2048]{0:T(1024)} %param.8) | copy-start | bytes 24580
  91.3 8.9 %collective-permute-start = (bf16[512,512]{1,0:T(8,128)(2,1)S(1)}, bf16[512,512]{1,0:T(8,128)(2,1)S(1)}, u32[]{:S(2)}, u32[]{:S(2)}) collective-permute-start(bf16[512,512]{1,0:T(8,128)(2,1)S(1)} %middle.1.refs_0_), channel_id=1, source_target_pairs={{0,1},{1,0},{2,3},{3,2},{4,5},{5,4},{6,7},{7,6},{8,9},{9,8},{10,11... | collective-permute-start | bytes 1572872 | tf_op jit(solution)/shard_map/ppermute | solution.py:334

commit v5 on v4

--- a/solution.py
+++ b/solution.py
@@ -102,7 +102,7 @@
     nx, ny = facet_scr.shape
     blocks = contrib // STEP
 
-    width = min(256, ny)
+    width = min(512, ny)
 
     def columns(at, carry):
         lanes = pl.ds(pl.multiple_of(at * width, width), width)
@@ -186,12 +186,11 @@
 
 
 def middle_kernel(
-    where_ref, lines_ref, a_hbm, kern_ref, counts_ref, e_ref, a_scr, w_scr, sems,
+    where_ref, lines_ref, a_ref, d_hbm, kern_ref, counts_ref, e_ref, d_ref, w_scr, sem,
     *, subs, per, contrib, tile,
 ):
-    loads = [pltpu.make_async_copy(a_hbm.at[s], a_scr.at[s], sems.at[s]) for s in range(per)]
-    for load in loads:
-        load.start()
+    bring = pltpu.make_async_copy(d_hbm, d_ref, sem)
+    bring.start()
     sub_at = where_ref[0] % subs
     tiles = contrib // tile
     k = kern_ref[...]
@@ -209,10 +208,10 @@
         w_scr[s, 1, contrib:, :] = (-wr).astype(jnp.bfloat16)
     total = None
     for s in range(per):
-        loads[s].wait()
-        here = nn(w_scr[s, 0], a_scr[s, 0]) + nn(w_scr[s, 1], a_scr[s, 1])
+        here = nn(w_scr[s, 0], a_ref[s, 0]) + nn(w_scr[s, 1], a_ref[s, 1])
         total = here if total is None else total + here
     e_ref[...] = total.T.astype(jnp.bfloat16)
+    bring.wait()
 
 
 def backward_kernel(mine_ref, other_ref, d_ref, window_ref, out_hbm, out_scr, sems, *, chunks):
@@ -297,8 +296,8 @@
             *refs, bands=bands, subs=subs, per=per, contrib=contrib, a_scale=a_scale, d_scale=d_scale,
         ),
         out_shape=(
-            pltpu.HBM((per, 2, contrib, nx), jnp.bfloat16),
-            pltpu.VMEM((2 * contrib, ny), jnp.bfloat16),
+            pltpu.VMEM((per, 2, contrib, nx), jnp.bfloat16),
+            pltpu.HBM((2 * contrib, ny), jnp.bfloat16),
         ),
         in_specs=[smem, smem, smem, smem, vmem, anywhere],
         out_specs=(vmem, vmem),
@@ -317,22 +316,24 @@
     grid = grid.reshape(2, per, contrib, contrib)
 
     counts = jnp.swapaxes(tile_counts, 1, 2).astype(jnp.bfloat16)
-    e_part = pl.pallas_call(
+    e_part, d_table = pl.pallas_call(
         lambda *refs: middle_kernel(*refs, subs=subs, per=per, contrib=contrib, tile=tile),
-        out_shape=pltpu.VMEM((nx, 2 * contrib), jnp.bfloat16),
-        in_specs=[smem, vmem, far, vmem, vmem],
-        out_specs=vmem,
+        out_shape=(
+            pltpu.VMEM((nx, 2 * contrib), jnp.bfloat16),
+            pltpu.VMEM((2 * contrib, ny), jnp.bfloat16),
+        ),
+        in_specs=[smem, vmem, vmem, far, vmem, vmem],
+        out_specs=(vmem, vmem),
         scratch_shapes=[
-            pltpu.VMEM((per, 2, contrib, nx), jnp.bfloat16),
             pltpu.VMEM((per, 2, 2 * contrib, contrib), jnp.bfloat16),
-            pltpu.SemaphoreType.DMA((per,)),
+            pltpu.SemaphoreType.DMA(()),
         ],
         compiler_params=pltpu.CompilerParams(vmem_limit_bytes=28 * 2**20),
         name="middle",
-    )(here, near(grid), distant(a_table), kernel, counts)
+    )(here, near(grid), near(a_table), distant(d_table), kernel, counts)
 
     other = lax.ppermute(e_part, "core", [(i, (i + 1) % subs) for i in range(subs)])
-    chunks = 8
+    chunks = 4
     return pl.pallas_call(
         lambda *refs: backward_kernel(*refs, chunks=chunks),
         out_shape=jax.ShapeDtypeStruct((nx, ny), jnp.bfloat16),

time: 103 us -> 101 us (0.981)
    pallas_call x1, Pallas kernels: 3.02 us -> 1.75 us  [body(): pl.pallas_call(lambda *refs: middle_kernel(*refs, subs=subs, per=per, con...]
where the time goes in v5:
time: 101 us
  blocking collectives  64.2 us (64%)
  Pallas kernels  15.2 us (15%)
  starting transfers between devices  11.1 us (11%)
  waiting for transfers between devices  8.45 us (8%)
  local copies, waits for them, and re-layouts  1.18 us (1%)
    all_to_all x3, blocking collectives, exchanged(): return lax.all_to_all(x, axes, 0, 0, tiled=True)  64.2 us
    ppermute x1, starting transfers between devices, body(): lax.ppermute(e_part, 'core', [(i, (i + 1) % subs) for i in range(subs)])  7.41 us
    all_to_all x1, waiting for transfers between devices, exchanged(): return lax.all_to_all(x, axes, 0, 0, tiled=True)  6.94 us
    pallas_call x1, Pallas kernels, body(): pl.pallas_call(lambda *refs: tables_kernel(*refs, bands=bands, subs=subs,...  6.28 us
    pallas_call x1, Pallas kernels, body(): pl.pallas_call(lambda *refs: forward_kernel(*refs, bands=bands, subs=subs...  5.04 us
    all_to_all x1, starting transfers between devices, exchanged(): return lax.all_to_all(x, axes, 0, 0, tiled=True)  3.65 us
    pallas_call x1, Pallas kernels, body(): pl.pallas_call(lambda *refs: backward_kernel(*refs, chunks=chunks), out_s...  2.1 us
  transfers between devices with their start and end apart: 2, of which 2 were waited for; matrix products, arithmetic and copies ran while one was open for 0% of the time, Pallas kernels for 6%

profile of v5, /device:TPU:1, one launch (start us, length us, event | category | flops | bytes accessed | tf_op | source)
XLA Modules:
  0.0 101.0 jit_solution(7734420261031936546)
XLA Ops:
  0.7 5.0 %forward.1 = bf16[2,4,256,256]{3,2,1,0:T(8,128)(2,1)S(1)} custom-call(s32[1]{0:T(128)} %bitcast.refs_0_, s32[1]{0:T(128)S(6)} %copy.9.refs_1_.refs_3_, s32[2,64]{1,0:T(2,128)} %bitcast.14, s32[8]{0:T(128)} %refs_2_.1, f32[1,2048]{1,0:T(1,128)} %bitcast.12, bf16[256,256]{1,0:T(8,128)(2,1)} %refs_4_.3, bf16[512,2048]{1,0:T(8,128)(2,1)} %refs_6_.1), custom_call_target="tpu_custom_call" | custom-call | tf_op jit(solution)/shard_map/forward/pallas_call | solution.py:270
  5.7 22.7 %all_to_all.20 = bf16[16,128,256]{2,1,0:T(8,128)(2,1)S(1)} all-to-all(bf16[16,128,256]{2,1,0:T(8,128)(2,1)S(1)} %bitcast.9), channel_id=1, replica_groups=mesh['y'=4,'zh'=4,'x'=4,'zl'=4,'core'=2] {'y','x'}, dimensions={0} | all-to-all | bytes 2097152 | tf_op jit(solution)/shard_map/all_to_all | solution.py:235
  28.4 0.0 copy-start.4
  28.4 0.1 reduce_sum.24.refs_5_
  28.6 0.0 copy-start
  28.6 0.0 copy-start.2
  28.6 0.0 copy-start.3
  28.6 27.1 %all_to_all.21 = bf16[16,8,256]{2,1,0:T(8,128)(2,1)S(1)} all-to-all(bf16[16,8,256]{2,1,0:T(8,128)(2,1)S(1)} %bitcast.11), channel_id=1, replica_groups=mesh['y'=4,'zh'=4,'x'=4,'zl'=4,'core'=2] {'zh','zl'}, dimensions={0} | all-to-all | bytes 131072 | tf_op jit(solution)/shard_map/all_to_all | solution.py:235
  55.8 14.4 %all_to_all.22 = bf16[16,8,256]{2,1,0:T(8,128)(2,1)S(1)} all-to-all(bf16[16,8,256]{2,1,0:T(8,128)(2,1)S(1)} %broadcast_in_dim.6), channel_id=1, replica_groups=mesh['y'=4,'zh'=4,'x'=4,'zl'=4,'core'=2] {'zh','zl'}, dimensions={0} | all-to-all | bytes 131072 | tf_op jit(solution)/shard_map/all_to_all | solution.py:235
  70.2 1.1 %broadcast_in_dim.7 = bf16[16,128,256]{2,1,0:T(8,128)(2,1)} broadcast(bf16[128,256]{1,0:T(8,128)(2,1)S(1)} %bitcast.16), dimensions={1,2} | broadcast | bytes 1114112 | tf_op jit(solution)/shard_map/broadcast_in_dim | solution.py:315
  71.2 3.7 %all-to-all-start.3 = ((bf16[16,128,256]{2,1,0:T(8,128)(2,1)}), bf16[16,128,256]{2,1,0:T(8,128)(2,1)S(1)}, u32[]{:S(2)}, u32[]{:S(2)}) async-start(bf16[16,128,256]{2,1,0:T(8,128)(2,1)} %broadcast_in_dim.7), calls=%async_computation.3 | async-start | bytes 2097152 | tf_op jit(solution)/shard_map/all_to_all | solution.py:235
  74.9 0.0 copy-done.4
  74.9 0.1 copy.8
  75.0 0.0 copy-done
  75.0 0.0 copy-done.2
  75.0 0.0 copy-done.3
  75.0 6.3 %tables.1 = (bf16[4,2,256,512]{3,2,1,0:T(8,128)(2,1)S(1)}, bf16[512,2048]{1,0:T(8,128)(2,1)}) custom-call(s32[1]{0:T(128)} %bitcast.refs_0_, s32[2,64]{1,0:T(2,128)S(1)} %bitcast.15, s32[8]{0:T(128)S(1)} %copy-done.3, s32[1]{0:T(128)S(6)} %copy.9.refs_1_.refs_3_, bf16[256,256]{1,0:T(8,128)(2,1)S(1)} %copy-done, bf16[128,256]{1,0:T(8,128)(2,1)S(1)} %reduce_sum.24.refs_5_), custom_call_target="tpu_custom_call" | custom-call | flops 6000000000 | bytes 4000000 | tf_op jit(solution)/shard_map/tables/pallas_call | solution.py:294
  81.3 6.9 %all-to-all-done.3 = bf16[16,128,256]{2,1,0:T(8,128)(2,1)S(1)} async-done(((bf16[16,128,256]{2,1,0:T(8,128)(2,1)}), bf16[16,128,256]{2,1,0:T(8,128)(2,1)S(1)}, u32[]{:S(2)}, u32[]{:S(2)}) %all-to-all-start.3) | async-done | bytes 1048608 | tf_op jit(solution)/shard_map/all_to_all | solution.py:235
  88.3 0.0 copy-start.1
  88.3 1.7 %middle.1 = (bf16[512,512]{1,0:T(8,128)(2,1)S(1)}, bf16[512,2048]{1,0:T(8,128)(2,1)S(1)}) custom-call(s32[1]{0:T(128)} %bitcast.refs_0_, bf16[2,4,256,256]{3,2,1,0:T(8,128)(2,1)S(1)} %bitcast.10, bf16[4,2,256,512]{3,2,1,0:T(8,128)(2,1)S(1)} %get-tuple-element.9.refs_2_, bf16[512,2048]{1,0:T(8,128)(2,1)} %get-tuple-element.10.refs_3_, ...), custom_call_target="tpu_custom_call" | custom-call | tf_op jit(solution)/shard_map/middle/pallas_call | solution.py:319
  90.0 7.4 %collective-permute-start = (bf16[512,512]{1,0:T(8,128)(2,1)S(1)}, bf16[512,512]{1,0:T(8,128)(2,1)S(1)}, u32[]{:S(2)}, u32[]{:S(2)}) collective-permute-start(bf16[512,512]{1,0:T(8,128)(2,1)S(1)} %get-tuple-element.11.refs_0_), channel_id=1, source_target_pairs={{0,1},{1,0},{2,3},{3,2},{4,5},{5,4},{6,7},{7,6},{8,9},{9,8},{10,11... | collective-permute-start | bytes 1572872 | tf_op jit(solution)/shard_map/ppermute | solution.py:335
  97.4 1.5 %collective-permute-done.refs_1_ = bf16[512,512]{1,0:T(8,128)(2,1)S(1)} collective-permute-done((bf16[512,512]{1,0:T(8,128)(2,1)S(1)}, bf16[512,512]{1,0:T(8,128)(2,1)S(1)}, u32[]{:S(2)}, u32[]{:S(2)}) %collective-permute-start) | collective-permute-done | bytes 524320 | tf_op jit(solution)/shard_map/ppermute | solution.py:335
  98.9 0.0 copy-done.1
  98.9 2.1 %backward.1 = bf16[512,2048]{1,0:T(8,128)(2,1)} custom-call(bf16[512,512]{1,0:T(8,128)(2,1)S(1)} %get-tuple-element.11.refs_0_, bf16[512,512]{1,0:T(8,128)(2,1)S(1)} %collective-permute-done.refs_1_, bf16[512,2048]{1,0:T(8,128)(2,1)S(1)} %get-tuple-element.12.refs_2_, f32[1,2048]{1,0:T(1,128)S(1)} %bitcast.13), custom_call_target="tpu_custom_call" | custom-call | tf_op jit(solution)/shard_map/backward/pallas_call | solution.py:337
  (3 shorter events, 0.0 us)
Async XLA Ops:
  28.4 46.5 %copy-start.4 = (s32[8,16,16]{2,1,0:T(8,128)S(1)}, s32[8,16,16]{2,1,0:T(8,128)}, u32[]{:S(2)}) copy-start(s32[8,16,16]{2,1,0:T(8,128)} %param.13) | copy-start | bytes 24580
  28.6 46.4 %copy-start = (bf16[256,256]{1,0:T(8,128)(2,1)S(1)}, bf16[256,256]{1,0:T(8,128)(2,1)}, u32[]{:S(2)}) copy-start(bf16[256,256]{1,0:T(8,128)(2,1)} %refs_4_.3) | copy-start | bytes 393220
  28.6 46.4 %copy-start.2 = (s32[64,2]{0,1:T(2,128)S(1)}, s32[64,2]{0,1:T(2,128)}, u32[]{:S(2)}) copy-start(s32[64,2]{0,1:T(2,128)} %param.9) | copy-start | bytes 1540
  28.6 46.4 %copy-start.3 = (s32[8]{0:T(128)S(1)}, s32[8]{0:T(128)}, u32[]{:S(2)}) copy-start(s32[8]{0:T(128)} %refs_2_.1) | copy-start | bytes 100
  71.2 17.0 %all-to-all-start.3 = ((bf16[16,128,256]{2,1,0:T(8,128)(2,1)}), bf16[16,128,256]{2,1,0:T(8,128)(2,1)S(1)}, u32[]{:S(2)}, u32[]{:S(2)}) async-start(bf16[16,128,256]{2,1,0:T(8,128)(2,1)} %broadcast_in_dim.7), calls=%async_computation.3 | async-start | bytes 2097152 | tf_op jit(solution)/shard_map/all_to_all | solution.py:235
  88.3 10.7 %copy-start.1 = (f32[2048]{0:T(1024)S(1)}, f32[2048]{0:T(1024)}, u32[]{:S(2)}) copy-start(f32[2048]{0:T(1024)} %param.8) | copy-start | bytes 24580
  90.0 8.9 %collective-permute-start = (bf16[512,512]{1,0:T(8,128)(2,1)S(1)}, bf16[512,512]{1,0:T(8,128)(2,1)S(1)}, u32[]{:S(2)}, u32[]{:S(2)}) collective-permute-start(bf16[512,512]{1,0:T(8,128)(2,1)S(1)} %get-tuple-element.11.refs_0_), channel_id=1, source_target_pairs={{0,1},{1,0},{2,3},{3,2},{4,5},{5,4},{6,7},{7,6},{8,9},{9,8},{10,11... | collective-permute-start | bytes 1572872 | tf_op jit(solution)/shard_map/ppermute | solution.py:335
